TPU v7x, 8 devices: a whole 2x2x1 slice. The times are simulated.
8 devices in a mesh: dp: 1 (over z), tp: 2 (over y), sp: 4 (over x, core).
Axes of the slice: x: 2, y: 2, z: 1, core: 2. Of those that a mesh axis runs over, the one named last changes fastest.
Arguments:
- hidden: bfloat16 [64, 3072], P('dp')
- positions: int32 [64], P('dp')
- k_cache: bfloat16 [2, 64, 256, 8, 128], P(None, 'dp', 'sp', 'tp')
- v_cache: bfloat16 [2, 64, 256, 8, 128], P(None, 'dp', 'sp', 'tp')
- ln_gain: bfloat16 [2, 2, 3072], replicated
- ln_bias: bfloat16 [2, 2, 3072], replicated
- w_qkv: bfloat16 [2, 3072, 5120], P(None, None, 'tp')
- b_qkv: bfloat16 [2, 5120], P(None, 'tp')
- w_dense: bfloat16 [2, 3072, 3072], P(None, 'tp')
- b_dense: bfloat16 [2, 3072], replicated
- w_up: bfloat16 [2, 3072, 16384], P(None, None, 'tp')
- b_up: bfloat16 [2, 16384], P(None, 'tp')
- w_down: bfloat16 [2, 8192, 3072], P(None, 'tp')
- b_down: bfloat16 [2, 3072], replicated
Outputs:
- output 1: bfloat16 [64, 3072], P('dp')
- output 2: bfloat16 [2, 64, 256, 8, 128], P(None, 'dp', 'sp', 'tp')
- output 3: bfloat16 [2, 64, 256, 8, 128], P(None, 'dp', 'sp', 'tp')
All inputs are finite; a program needn't handle non-finite values.
Results may differ from a plain program's by a relative error of at most 0.017098.
Values sent between devices are 32-bit elements.
A program may use at most 1 GiB of HBM per device.

v0:
```python
import functools
import math

import jax
import jax.numpy as jnp
from jax import lax
from jax.experimental import pallas as pl
from jax.experimental.pallas import tpu as pltpu
from jax.sharding import PartitionSpec as P

BLOCK_SIZE = 64
LOCAL_BLOCKS = 16
VERT_STRIDE = 8
ROPE_THETA = 1000000.0
GELU_LIMIT = 20.0
NORM_EPS = 0.00001
MASKED = -1e30
MESH = pl.DeviceIdType.MESH

NB = 64
D = 3072
HD = 128
KVL = 4
GRP = 3
SLOTS = 64
QW = KVL * (GRP + 2) * HD
QROWS = 16
KCH = 6
KCS = D // KCH
G = 8
NG = NB // G
HALF = NB // 2
HPC = 6
MSG = HPC * HALF + 8
ROWS = HALF // 2
F_LOC = 4096
M_LOC = F_LOC // 2
NCH = 4
CW = D // NCH
DR = HPC * HD
LAG = 2
VMEM_BYTES = 52 * 1024 * 1024

f32 = jnp.float32
bf16 = jnp.bfloat16


def norm_rows(rows, gain, shift):
    mean = jnp.mean(rows, axis=-1, keepdims=True)
    cent = rows - mean
    var = jnp.mean(jnp.square(cent), axis=-1, keepdims=True)
    return (cent * lax.rsqrt(var + NORM_EPS)) * gain + shift


def rope_tables(pos):
    half = HD // 2
    row = lax.broadcasted_iota(jnp.int32, (8, HD), 0)
    lane = lax.broadcasted_iota(jnp.int32, (NB, HD), 1)
    groups = []
    for i in range(NB // 8):
        at = jnp.zeros((8, HD), jnp.int32)
        for r in range(8):
            at = jnp.where(row == r, pos[i * 8 + r], at)
        groups.append(at)
    where = jnp.concatenate(groups, axis=0).astype(f32)
    power = (lane % half).astype(f32) * (2.0 / HD)
    angles = where * jnp.exp(power * -math.log(ROPE_THETA))
    sin = jnp.sin(angles)
    return jnp.cos(angles), jnp.where(lane < half, -sin, sin)


def attn_kernel(layer, pos, x, gain, shift, b_qkv, w_hbm, kc_hbm, vc_hbm, *rest):
    if layer == 1:
        rest = rest[2:]
    (msg, ko_hbm, vo_hbm, w, kbuf, vbuf, u, acc, qs, kns, vns, os, ms, ls, wsem, ksem, vsem, osem) = rest[:18]
    sp = lax.axis_index('sp')
    tp = lax.axis_index('tp')
    base = sp * SLOTS

    def w_copy(i):
        return pltpu.make_async_copy(w_hbm.at[layer, pl.ds(i * KCS, KCS), :], w.at[i], wsem.at[i])

    def in_copy(hbm, buf, sem, i):
        return pltpu.make_async_copy(hbm.at[layer, pl.ds(i * G, G)], buf.at[pl.ds(i * G, G)], sem.at[i])

    def out_copy(buf, hbm, j, i):
        return pltpu.make_async_copy(buf.at[pl.ds(i * G, G)], hbm.at[layer, pl.ds(i * G, G)], osem.at[j, i])

    if layer == 0:
        places, small_sem = rest[18:23], rest[23]
        small = [pltpu.make_async_copy(src, dst, small_sem.at[i]) for i, (src, dst) in enumerate(zip((pos, x, gain, shift, b_qkv), places))]
        for copy in small:
            copy.start()
        pos, x, gain, shift, b_qkv = places
    for i in range(KCH):
        w_copy(i).start(priority=i % 2)
    for i in range(NG):
        in_copy(kc_hbm, kbuf, ksem, i).start(priority=0)
        in_copy(vc_hbm, vbuf, vsem, i).start(priority=1)
    if layer == 0:
        for copy in small:
            copy.wait()

    g_row = gain[layer, 0:1, :].astype(f32)
    s_row = shift[layer, 0:1, :].astype(f32)
    for i in range(NB // 16):
        rows = x[pl.ds(i * 16, 16), :].astype(f32)
        normed = norm_rows(rows, g_row, s_row).astype(bf16)
        for j in range(KCH):
            u[j, pl.ds(i * 16, 16), :] = normed[:, j * KCS:(j + 1) * KCS]
    acc[...] = jnp.broadcast_to(b_qkv[layer:layer + 1, :].astype(f32), (NB, QW))
    qs[...] = jnp.zeros_like(qs)

    cos_t, sin_t = rope_tables(pos)

    def qkv_step(i, carry):
        w_copy(i).wait()
        acc[...] += jnp.dot(u[i], w[i], preferred_element_type=f32)
        return carry

    lax.fori_loop(0, KCH, qkv_step, 0)

    for c in range(KVL):
        for j in range(GRP + 2):
            col = (c * (GRP + 2) + j) * HD
            tile = acc[:, col:col + HD]
            if j <= GRP:
                tile = tile * cos_t + pltpu.roll(tile, HD // 2, 1) * sin_t
            for i in range(NB // 8):
                part = tile[i * 8:(i + 1) * 8]
                if j < GRP:
                    qs[pl.ds(i * 8 * QROWS + c * GRP + j, 8, stride=QROWS), :] = part
                else:
                    dst = kns if j == GRP else vns
                    dst[pl.ds(i * 64 + c, 8, stride=8), :] = part
                    dst[pl.ds(i * 64 + c + 4, 8, stride=8), :] = part

    row_h = lax.broadcasted_iota(jnp.int32, (QROWS, SLOTS * KVL), 0)
    col_i = lax.broadcasted_iota(jnp.int32, (QROWS, SLOTS * KVL), 1)
    slot_of = jnp.where(row_h // GRP == col_i % KVL, col_i // KVL, 1 << 20)
    head_id = tp * KVL * GRP + row_h
    vertical = (sp + head_id + 1) % VERT_STRIDE == 0
    sub_row = lax.broadcasted_iota(jnp.int32, (16, HD), 0) // KVL

    def attn_step(i, carry):
        in_copy(kc_hbm, kbuf, ksem, i).wait()
        in_copy(vc_hbm, vbuf, vsem, i).wait()
        limits = []
        for bi in range(G):
            b = i * G + bi
            p = pos[b]
            pl_ = p - base
            pc = jnp.clip(pl_, 0, SLOTS - 1)
            hit = jnp.logical_and(pl_ >= 0, pl_ < SLOTS)
            sub = jnp.where(hit, pc % KVL, -1)
            r0 = pl.multiple_of((pc // KVL) * 16, 16)
            put = sub_row == sub
            for buf, new in ((kbuf, kns), (vbuf, vns)):
                new8 = new[pl.ds(pl.multiple_of(b * 8, 8), 8), :]
                new16 = jnp.concatenate([new8, new8], axis=0)
                old = buf[b, pl.ds(r0, 16), :].astype(f32)
                buf[b, pl.ds(r0, 16), :] = jnp.where(put, new16, old).astype(bf16)
            if layer == 0:
                near = p // BLOCK_SIZE - sp < LOCAL_BLOCKS
                limits.append(jnp.where(vertical, pl_, jnp.where(near, pl_, -1)))
            else:
                limits.append(pl_)
        scores = []
        for bi in range(G):
            b = i * G + bi
            q = qs[pl.ds(pl.multiple_of(b * QROWS, QROWS), QROWS), :].astype(bf16)
            scores.append(lax.dot_general(q, kbuf[b], (((1,), (1,)), ((), ())), preferred_element_type=f32))
        keeps = [slot_of <= limit for limit in limits]
        scores = [jnp.where(keep, s * (1.0 / HD), MASKED) for keep, s in zip(keeps, scores)]
        peaks = [jnp.max(s, axis=1, keepdims=True) for s in scores]
        weights = [jnp.where(keep, jnp.exp(s - peak), 0.0) for keep, s, peak in zip(keeps, scores, peaks)]
        outs = [jnp.dot(wt.astype(bf16), vbuf[i * G + bi], preferred_element_type=f32) for bi, wt in enumerate(weights)]
        sums = [jnp.sum(wt, axis=1, keepdims=True) for wt in weights]
        for bi in range(G):
            rows = pl.ds(pl.multiple_of((i * G + bi) * QROWS, QROWS), QROWS)
            ms[rows, :] = jnp.broadcast_to(peaks[bi], (QROWS, HD))
            ls[rows, :] = jnp.broadcast_to(sums[bi], (QROWS, HD))
            os[rows, :] = outs[bi]

        @pl.when(i > 0)
        def _():
            out_copy(kbuf, ko_hbm, 0, i - 1).start()
            out_copy(vbuf, vo_hbm, 1, i - 1).start(priority=1)

        return carry

    lax.fori_loop(0, NG, attn_step, 0)

    lane = lax.broadcasted_iota(jnp.int32, (8, HD), 1)
    for half in range(2):
        for c in range(2):
            stat = jnp.zeros((8, HD), f32)
            for g in range(HPC):
                for i in range(HALF // 8):
                    rows = pl.ds((half * HALF + i * 8) * QROWS + c * HPC + g, 8, stride=QROWS)
                    at = 2 * (g * (HALF // 8) + i)
                    msg[half * 2 + c, pl.ds(g * HALF + i * 8, 8), :] = os[rows, :]
                    stat = jnp.where(lane == at, ms[rows, :], stat)
                    stat = jnp.where(lane == at + 1, ls[rows, :], stat)
            msg[half * 2 + c, pl.ds(HPC * HALF, 8), :] = stat
    out_copy(kbuf, ko_hbm, 0, NG - 1).start()
    out_copy(vbuf, vo_hbm, 1, NG - 1).start(priority=1)
    for i in range(NG):
        out_copy(kbuf, ko_hbm, 0, i).wait()
        out_copy(vbuf, vo_hbm, 1, i).wait()


def attn_call(layer, pos, x, gain, shift, b_qkv, w_qkv, k_cache, v_cache, prev):
    vm = pl.BlockSpec(memory_space=pltpu.VMEM)
    hbm = pl.BlockSpec(memory_space=pltpu.HBM)
    args = [pos, x, gain, shift, b_qkv, w_qkv, k_cache, v_cache]
    if layer == 0:
        specs = [hbm] * 8
        alias = {}
        small = [pltpu.SMEM(pos.shape, jnp.int32)] + [pltpu.VMEM(arr.shape, bf16) for arr in (x, gain, shift, b_qkv)]
        small.append(pltpu.SemaphoreType.DMA((5,)))
        limit = 60 * 1024 * 1024
    else:
        args += list(prev)
        specs = [pl.BlockSpec(memory_space=pltpu.SMEM)] + [vm] * 4 + [hbm] * 5
        alias = {8: 1, 9: 2}
        small = []
        limit = VMEM_BYTES
    cache = jax.ShapeDtypeStruct(k_cache.shape, bf16)
    return pl.pallas_call(
        functools.partial(attn_kernel, layer),
        out_shape=(jax.ShapeDtypeStruct((KVL, MSG, HD), f32), cache, cache),
        in_specs=specs,
        out_specs=(vm, hbm, hbm),
        scratch_shapes=[
            pltpu.VMEM((KCH, KCS, QW), bf16),
            pltpu.VMEM((NB, SLOTS * KVL, HD), bf16),
            pltpu.VMEM((NB, SLOTS * KVL, HD), bf16),
            pltpu.VMEM((KCH, NB, KCS), bf16),
            pltpu.VMEM((NB, QW), f32),
            pltpu.VMEM((NB * QROWS, HD), f32),
            pltpu.VMEM((NB * 8, HD), f32),
            pltpu.VMEM((NB * 8, HD), f32),
            pltpu.VMEM((NB * QROWS, HD), f32),
            pltpu.VMEM((NB * QROWS, HD), f32),
            pltpu.VMEM((NB * QROWS, HD), f32),
            pltpu.SemaphoreType.DMA((KCH,)),
            pltpu.SemaphoreType.DMA((NG,)),
            pltpu.SemaphoreType.DMA((NG,)),
            pltpu.SemaphoreType.DMA((2, NG)),
            *small,
        ],
        input_output_aliases=alias,
        compiler_params=pltpu.CompilerParams(vmem_limit_bytes=limit),
        name=f'attn{layer}',
    )(*args)


def rest_kernel(layer, msg, x, gain, shift, b_dense, b_up, b_down, wd_hbm, wu_hbm, wn_hbm, out,
                wd, wu, wn, got, sent, o_buf, part, pair, sums, other, ag, full, xrow, up, mbuf,
                wsem, a_sem, d_sem, y_sem, g_sem, x_sem):
    dp = lax.axis_index('dp')
    tp = lax.axis_index('tp')
    sp = lax.axis_index('sp')
    core = sp % 2
    cx = sp // 2
    ox = 1 - cx
    mate = (dp, tp, cx * 2 + 1 - core)
    x_dev = (dp, tp, ox * 2 + core)
    y_dev = (dp, 1 - tp, sp)

    def load(src, dst, i):
        return pltpu.make_async_copy(src, dst, wsem.at[i])

    wd_copy = load(wd_hbm.at[layer, pl.ds(pl.multiple_of(core * DR, DR), DR), :], wd, 0)

    def wu_copy(i):
        return load(wu_hbm.at[layer, pl.ds(i * CW, CW), pl.ds(pl.multiple_of(core * F_LOC, F_LOC), F_LOC)], wu.at[i], 1 + i)

    wn_copy = load(wn_hbm.at[layer, pl.ds(pl.multiple_of(core * M_LOC, M_LOC), M_LOC), :], wn, 1 + NCH)

    barrier = pltpu.get_barrier_semaphore()
    for peer in (mate, x_dev, y_dev):
        pl.semaphore_signal(barrier, inc=1, device_id=peer, device_id_type=MESH)
    wd_copy.start()
    for i in range(NCH):
        wu_copy(i).start()
    wn_copy.start()
    pl.semaphore_wait(barrier, 3)

    def remote(src, dst, sems, idx, peer):
        return pltpu.make_async_remote_copy(
            src_ref=src, dst_ref=dst, send_sem=sems.at[(0,) + idx], recv_sem=sems.at[(1,) + idx],
            device_id=peer, device_id_type=MESH)

    near = cx * 2 + core
    far = ox * 2 + core
    swap = [remote(msg.at[ox * 2 + 1 - core], got.at[0], a_sem, (0,), mate),
            remote(msg.at[cx * 2 + 1 - core], got.at[1], a_sem, (1,), mate)]
    for copy in swap:
        copy.start()

    gain1 = gain[layer, 1:2, :].astype(f32)
    shift1 = shift[layer, 1:2, :].astype(f32)
    own = pl.ds(pl.multiple_of(core * ROWS, ROWS), ROWS)
    theirs = pl.ds(pl.multiple_of((1 - core) * ROWS, ROWS), ROWS)

    def all_rows(x_, c_):
        return pl.ds(pl.multiple_of(x_ * HALF + c_ * ROWS, ROWS), ROWS)

    xrow[...] = x[all_rows(cx, core), :].astype(f32)
    lane = lax.broadcasted_iota(jnp.int32, (8, HD), 1)

    def merge(one, two, put, stat_out=None):
        stats = [ref[pl.ds(HPC * HALF, 8), :] for ref in (one, two)]
        new_stat = jnp.zeros((8, HD), f32)
        for g in range(HPC):
            for i in range(HALF // 8):
                at = 2 * (g * (HALF // 8) + i)
                peaks = [jnp.broadcast_to(st[:, at:at + 1], (8, HD)) for st in stats]
                tots = [jnp.broadcast_to(st[:, at + 1:at + 2], (8, HD)) for st in stats]
                top = jnp.maximum(peaks[0], peaks[1])
                scale = [jnp.exp(p - top) for p in peaks]
                rows = pl.ds(g * HALF + i * 8, 8)
                num = one[rows, :] * scale[0] + two[rows, :] * scale[1]
                den = tots[0] * scale[0] + tots[1] * scale[1]
                put(g, i, num, den)
                if stat_out is not None:
                    new_stat = jnp.where(lane == at, top, new_stat)
                    new_stat = jnp.where(lane == at + 1, den, new_stat)
        if stat_out is not None:
            stat_out[pl.ds(HPC * HALF, 8), :] = new_stat

    def put_part(ref):
        def put(g, i, num, den):
            ref[pl.ds(g * HALF + i * 8, 8), :] = num
        return put

    def put_out(g, i, num, den):
        o_buf[pl.ds(i * 8, 8), g * HD:(g + 1) * HD] = num / den

    swap[0].wait_recv()
    merge(msg.at[far], got.at[0], put_part(sent.at[0]), sent.at[0])
    cross = remote(sent.at[0], got.at[2], a_sem, (2,), x_dev)
    cross.start()
    swap[1].wait_recv()
    merge(msg.at[near], got.at[1], put_part(sent.at[1]), sent.at[1])
    cross.wait_recv()
    merge(sent.at[1], got.at[2], put_out)
    for copy in swap + [cross]:
        copy.wait_send()

    def reduce(ph, product, finish):
        first = [remote(part.at[ph, n, theirs, :], pair.at[ph, n], d_sem, (ph, n), mate) for n in range(NCH)]
        second = [remote(sums.at[ph, n], other.at[ph, n], y_sem, (ph, n), y_dev) for n in range(NCH)]
        for step in range(NCH + LAG):
            if step < NCH:
                part[ph, step] = product(step)
                first[step].start()
            if step >= LAG:
                n = step - LAG
                first[n].wait_recv()
                sums[ph, n] = part[ph, n, own, :] + pair[ph, n]
                second[n].start()
        for n in range(NCH):
            second[n].wait_recv()
            finish(n, sums[ph, n] + other[ph, n])
        return first + second

    def residual(n, total, bias):
        cols = slice(n * CW, (n + 1) * CW)
        v = xrow[:, cols] + total + bias[layer:layer + 1, cols].astype(f32)
        xrow[:, cols] = v.astype(bf16).astype(f32)

    wd_copy.wait()
    o = o_buf[...].astype(bf16)
    sends = reduce(0, lambda n: jnp.dot(o, wd[:, n * CW:(n + 1) * CW], preferred_element_type=f32),
                   lambda n, total: residual(n, total, b_dense))

    normed = norm_rows(xrow[...], gain1, shift1).astype(bf16).astype(f32)
    swap = []
    for n in range(NCH):
        ag[n, own, :] = normed[:, n * CW:(n + 1) * CW]
        here = ag.at[n, own, :]
        swap.append(remote(here, here, g_sem, (n,), mate))
        swap[n].start()
    cols_up = pl.ds(pl.multiple_of(core * F_LOC, F_LOC), F_LOC)
    up[...] = jnp.broadcast_to(b_up[layer:layer + 1, cols_up].astype(f32), (HALF, F_LOC))
    for n in range(NCH):
        wu_copy(n).wait()
        swap[n].wait_recv()
        up[...] += jnp.dot(ag[n].astype(bf16), wu[n], preferred_element_type=f32)

    pick = (lax.broadcasted_iota(jnp.int32, (256, 128), 0) == 2 * lax.broadcasted_iota(jnp.int32, (256, 128), 1))
    pick = jnp.where(pick, 1.0, 0.0).astype(bf16)
    for k in range(F_LOC // 256):
        a = up[:, k * 256:(k + 1) * 256]
        z = jnp.minimum(a, GELU_LIMIT)
        gate = z * jax.nn.sigmoid(1.702 * z)
        lin = jnp.clip(a, -GELU_LIMIT, GELU_LIMIT) + 1.0
        prod = (gate * pltpu.roll(lin, 255, 1)).astype(bf16)
        mbuf[:, k * 128:(k + 1) * 128] = jnp.dot(prod, pick, preferred_element_type=f32).astype(bf16)
    wn_copy.wait()
    m = mbuf[...]
    sends += swap

    def spread(n, total):
        residual(n, total, b_down)
        full[n, all_rows(cx, core), :] = xrow[:, n * CW:(n + 1) * CW]
        here = full.at[n, all_rows(cx, core), :]
        for k, peer in enumerate((x_dev, mate)):
            copy = remote(here, here, x_sem, (k, n), peer)
            copy.start()
            sends.append(copy)

    sends += reduce(1, lambda n: jnp.dot(m, wn[:, n * CW:(n + 1) * CW], preferred_element_type=f32), spread)
    for n in range(NCH):
        there = full.at[n, all_rows(ox, core), :]
        remote(there, there, x_sem, (0, n), x_dev).wait_recv()
        copy = remote(there, there, x_sem, (2, n), mate)
        copy.start()
        sends.append(copy)
    for n in range(NCH):
        for k, x_ in ((1, cx), (2, ox)):
            there = full.at[n, all_rows(x_, 1 - core), :]
            remote(there, there, x_sem, (k, n), mate).wait_recv()
        out[:, n * CW:(n + 1) * CW] = full[n].astype(bf16)
    for copy in sends:
        copy.wait_send()


def rest_call(layer, msg, x, gain, shift, b_dense, b_up, b_down, w_dense, w_up, w_down):
    vm = pl.BlockSpec(memory_space=pltpu.VMEM)
    hbm = pl.BlockSpec(memory_space=pltpu.HBM)
    return pl.pallas_call(
        functools.partial(rest_kernel, layer),
        out_shape=jax.ShapeDtypeStruct((NB, D), bf16),
        in_specs=[vm] * 7 + [hbm] * 3,
        out_specs=vm,
        scratch_shapes=[
            pltpu.VMEM((DR, D), bf16),
            pltpu.VMEM((NCH, CW, F_LOC), bf16),
            pltpu.VMEM((M_LOC, D), bf16),
            pltpu.VMEM((3, MSG, HD), f32),
            pltpu.VMEM((2, MSG, HD), f32),
            pltpu.VMEM((HALF, DR), f32),
            pltpu.VMEM((2, NCH, HALF, CW), f32),
            pltpu.VMEM((2, NCH, ROWS, CW), f32),
            pltpu.VMEM((2, NCH, ROWS, CW), f32),
            pltpu.VMEM((2, NCH, ROWS, CW), f32),
            pltpu.VMEM((NCH, HALF, CW), f32),
            pltpu.VMEM((NCH, NB, CW), f32),
            pltpu.VMEM((ROWS, D), f32),
            pltpu.VMEM((HALF, F_LOC), f32),
            pltpu.VMEM((HALF, M_LOC), bf16),
            pltpu.SemaphoreType.DMA((2 + NCH,)),
            pltpu.SemaphoreType.DMA((2, 3)),
            pltpu.SemaphoreType.DMA((2, 2, NCH)),
            pltpu.SemaphoreType.DMA((2, 2, NCH)),
            pltpu.SemaphoreType.DMA((2, NCH)),
            pltpu.SemaphoreType.DMA((2, 3, NCH)),
        ],
        compiler_params=pltpu.CompilerParams(vmem_limit_bytes=VMEM_BYTES, collective_id=layer, has_side_effects=True),
        name=f'rest{layer}',
    )(msg, x, gain, shift, b_dense, b_up, b_down, w_dense, w_up, w_down)


def solution(mesh):
    cache_spec = P(None, 'dp', 'sp', 'tp', None)
    in_specs = (P('dp', None), P('dp'), cache_spec, cache_spec, P(), P(), P(None, None, 'tp'), P(None, 'tp'), P(None, 'tp', None), P(), P(None, None, 'tp'), P(None, 'tp'), P(None, 'tp', None), P())
    out_specs = (P('dp', None), cache_spec, cache_spec)

    def device_step(hidden, positions, k_cache, v_cache, ln_gain, ln_bias, w_qkv, b_qkv, w_dense, b_dense, w_up, b_up, w_down, b_down):
        shape = k_cache.shape
        flat = (2, NB, SLOTS * KVL, HD)
        k_cache = k_cache.reshape(flat)
        v_cache = v_cache.reshape(flat)
        caches = None
        for layer in range(2):
            msg, *caches = attn_call(layer, positions, hidden, ln_gain, ln_bias, b_qkv, w_qkv, k_cache, v_cache, caches)
            hidden = rest_call(layer, msg, hidden, ln_gain, ln_bias, b_dense, b_up, b_down, w_dense, w_up, w_down)
        return hidden, caches[0].reshape(shape), caches[1].reshape(shape)

    return jax.shard_map(device_step, mesh=mesh, in_specs=in_specs, out_specs=out_specs, check_vma=False)
```

profile of v0, /device:TPU:0, one launch (start us, length us, event | category | flops | bytes accessed | tf_op | source)
XLA Modules:
  0.0 102.4 jit_solution(2153443361444190642)
XLA Ops:
  0.6 0.0 copy-start
  0.6 0.0 copy-start.2
  0.7 0.0 copy-start.3
  0.7 0.0 copy-start.4
  0.7 0.0 copy-start.5
  0.7 0.0 copy-start.6
  0.7 15.4 %attn0.1 = (f32[4,200,128]{2,1,0:T(8,128)}, bf16[2,64,256,128]{3,2,1,0:T(8,128)(2,1)}, bf16[2,64,256,128]{3,2,1,0:T(8,128)(2,1)}) custom-call(s32[64]{0:T(128)} %pos.3, bf16[64,3072]{1,0:T(8,128)(2,1)} %x.3, bf16[2,2,3072]{2,1,0:T(2,128)(2,1)} %gain.7, bf16[2,2,3072]{2,1,0:T(2,128)(2,1)} %shift.7, bf16[2,2560]{1,0:T(2,128)(2,1)} %b_qkv.3, ...), custom_call_target="tpu_custom_call" | custom-call | tf_op jit(solution)/shard_map/attn0/pallas_call | solution.py:230
  16.1 0.0 copy-done
  16.2 0.0 copy-done.2
  16.2 0.0 copy-done.3
  16.2 0.0 copy-done.4
  16.2 0.0 copy-done.5
  16.2 0.0 copy-done.6
  16.2 0.0 copy-start.1
  16.2 1.0 copy-done.1
  17.2 0.0 copy-start.7
  17.2 0.0 copy-start.8
  17.2 35.4 %rest0.1.x = bf16[64,3072]{1,0:T(8,128)(2,1)S(1)} custom-call(f32[4,200,128]{2,1,0:T(8,128)S(1)} %copy-done.1, bf16[64,3072]{1,0:T(8,128)(2,1)S(1)} %copy-done, bf16[2,2,3072]{2,1,0:T(2,128)(2,1)S(1)} %copy-done.2, bf16[2,2,3072]{2,1,0:T(2,128)(2,1)S(1)} %copy-done.3, bf16[2,3072]{1,0:T(2,128)(2,1)S(1)} %copy-done.5, bf16[2,8192]{1,0:T(2,128)(2,1)S(1)} %copy-done.4, ...), custom_call_target="tpu_custom_call" | custom-call | tf_op jit(solution)/shard_map/rest0/pallas_call | solution.py:435
  52.6 0.0 copy-done.7
  52.6 0.0 copy-done.8
  52.6 14.8 %attn1.1 = (f32[4,200,128]{2,1,0:T(8,128)S(1)}, bf16[2,64,256,128]{3,2,1,0:T(8,128)(2,1)}, bf16[2,64,256,128]{3,2,1,0:T(8,128)(2,1)}) custom-call(s32[64]{0:T(128)S(1)} %copy-done.8, bf16[64,3072]{1,0:T(8,128)(2,1)S(1)} %rest0.1.x, bf16[2,2,3072]{2,1,0:T(2,128)(2,1)S(1)} %copy-done.2, ...), custom_call_target="tpu_custom_call", output_to_operand_aliasing={{1}: (8, {}), {2}: (9, {})} | custom-call | tf_op jit(solution)/shard_map/attn1/pallas_call | solution.py:230
  67.4 34.2 %rest1.1 = bf16[64,3072]{1,0:T(8,128)(2,1)S(1)} custom-call(f32[4,200,128]{2,1,0:T(8,128)S(1)} %get-tuple-element.12.msg, bf16[64,3072]{1,0:T(8,128)(2,1)S(1)} %rest0.1.x, bf16[2,2,3072]{2,1,0:T(2,128)(2,1)S(1)} %copy-done.2, bf16[2,2,3072]{2,1,0:T(2,128)(2,1)S(1)} %copy-done.3, bf16[2,3072]{1,0:T(2,128)(2,1)S(1)} %copy-done.5, ...), custom_call_target="tpu_custom_call" | custom-call | tf_op jit(solution)/shard_map/rest1/pallas_call | solution.py:435
  101.7 0.7 copy.22
Async XLA Ops:
  0.6 15.5 %copy-start = (bf16[64,3072]{1,0:T(8,128)(2,1)S(1)}, bf16[64,3072]{1,0:T(8,128)(2,1)}, u32[]{:S(2)}) copy-start(bf16[64,3072]{1,0:T(8,128)(2,1)} %x.3) | copy-start | bytes 1179652
  0.6 15.5 %copy-start.2 = (bf16[2,2,3072]{2,1,0:T(2,128)(2,1)S(1)}, bf16[2,2,3072]{2,1,0:T(2,128)(2,1)}, u32[]{:S(2)}) copy-start(bf16[2,2,3072]{2,1,0:T(2,128)(2,1)} %gain.7) | copy-start | bytes 73732
  0.7 15.5 %copy-start.3 = (bf16[2,2,3072]{2,1,0:T(2,128)(2,1)S(1)}, bf16[2,2,3072]{2,1,0:T(2,128)(2,1)}, u32[]{:S(2)}) copy-start(bf16[2,2,3072]{2,1,0:T(2,128)(2,1)} %shift.7) | copy-start | bytes 73732
  0.7 15.5 %copy-start.4 = (bf16[2,8192]{1,0:T(2,128)(2,1)S(1)}, bf16[2,8192]{1,0:T(2,128)(2,1)}, u32[]{:S(2)}) copy-start(bf16[2,8192]{1,0:T(2,128)(2,1)} %b_up.3) | copy-start | bytes 98308
  0.7 15.5 %copy-start.5 = (bf16[2,3072]{1,0:T(2,128)(2,1)S(1)}, bf16[2,3072]{1,0:T(2,128)(2,1)}, u32[]{:S(2)}) copy-start(bf16[2,3072]{1,0:T(2,128)(2,1)} %b_dense.3) | copy-start | bytes 36868
  0.7 15.5 %copy-start.6 = (bf16[2,3072]{1,0:T(2,128)(2,1)S(1)}, bf16[2,3072]{1,0:T(2,128)(2,1)}, u32[]{:S(2)}) copy-start(bf16[2,3072]{1,0:T(2,128)(2,1)} %b_down.3) | copy-start | bytes 36868
  16.2 1.0 copy-start.1
  17.2 35.4 %copy-start.7 = (bf16[2,2560]{1,0:T(2,128)(2,1)S(1)}, bf16[2,2560]{1,0:T(2,128)(2,1)}, u32[]{:S(2)}) copy-start(bf16[2,2560]{1,0:T(2,128)(2,1)} %b_qkv.3) | copy-start | bytes 30724
  17.2 35.4 %copy-start.8 = (s32[64]{0:T(128)S(1)}, s32[64]{0:T(128)}, u32[]{:S(2)}) copy-start(s32[64]{0:T(128)} %pos.3) | copy-start | bytes 772
where the time goes:
time: 103 us; the launch traced here: 102 us
  Pallas kernels  99.9 us (97%)
  local copies, waits for them, and re-layouts  1.78 us (2%)
    pallas_call x2, Pallas kernels, rest_call(): pl.pallas_call(functools.partial(rest_kernel, layer), out_shape=jax.Shape...  69.7 us
    pallas_call x2, Pallas kernels, attn_call(): pl.pallas_call(functools.partial(attn_kernel, layer), out_shape=(jax.Shap...  30.2 us

commit v1 on v0

--- a/solution.py
+++ b/solution.py
@@ -37,6 +37,7 @@
 M_LOC = F_LOC // 2
 NCH = 4
 CW = D // NCH
+QC = QW // NCH
 DR = HPC * HD
 LAG = 2
 VMEM_BYTES = 52 * 1024 * 1024
@@ -69,61 +70,69 @@
     return jnp.cos(angles), jnp.where(lane < half, -sin, sin)
 
 
-def attn_kernel(layer, pos, x, gain, shift, b_qkv, w_hbm, kc_hbm, vc_hbm, *rest):
-    if layer == 1:
-        rest = rest[2:]
-    (msg, ko_hbm, vo_hbm, w, kbuf, vbuf, u, acc, qs, kns, vns, os, ms, ls, wsem, ksem, vsem, osem) = rest[:18]
+def attn_kernel(layer, pos, *rest):
+    if layer == 0:
+        x, gain, shift, b_qkv, w_hbm, kc_hbm, vc_hbm, *rest = rest
+    else:
+        acc, kc_hbm, vc_hbm, _, _, *rest = rest
+    msg, ko_hbm, vo_hbm, kbuf, vbuf, qs, kns, vns, os, ms, ls, ksem, vsem, osem, *rest = rest
     sp = lax.axis_index('sp')
     tp = lax.axis_index('tp')
     base = sp * SLOTS
 
-    def w_copy(i):
-        return pltpu.make_async_copy(w_hbm.at[layer, pl.ds(i * KCS, KCS), :], w.at[i], wsem.at[i])
-
     def in_copy(hbm, buf, sem, i):
         return pltpu.make_async_copy(hbm.at[layer, pl.ds(i * G, G)], buf.at[pl.ds(i * G, G)], sem.at[i])
 
     def out_copy(buf, hbm, j, i):
         return pltpu.make_async_copy(buf.at[pl.ds(i * G, G)], hbm.at[layer, pl.ds(i * G, G)], osem.at[j, i])
 
-    if layer == 0:
-        places, small_sem = rest[18:23], rest[23]
+    def fetch_cache():
+        for i in range(NG):
+            in_copy(kc_hbm, kbuf, ksem, i).start(priority=0)
+            in_copy(vc_hbm, vbuf, vsem, i).start(priority=1)
+
+    if layer == 0:
+        w, u, acc, wsem, *places, small_sem = rest
         small = [pltpu.make_async_copy(src, dst, small_sem.at[i]) for i, (src, dst) in enumerate(zip((pos, x, gain, shift, b_qkv), places))]
         for copy in small:
             copy.start()
         pos, x, gain, shift, b_qkv = places
-    for i in range(KCH):
-        w_copy(i).start(priority=i % 2)
-    for i in range(NG):
-        in_copy(kc_hbm, kbuf, ksem, i).start(priority=0)
-        in_copy(vc_hbm, vbuf, vsem, i).start(priority=1)
-    if layer == 0:
+
+        def w_copy(i):
+            return pltpu.make_async_copy(w_hbm.at[layer, pl.ds(i * KCS, KCS), :], w.at[i], wsem.at[i])
+
+        for i in range(KCH):
+            w_copy(i).start(priority=i % 2)
+        fetch_cache()
         for copy in small:
             copy.wait()
-
-    g_row = gain[layer, 0:1, :].astype(f32)
-    s_row = shift[layer, 0:1, :].astype(f32)
-    for i in range(NB // 16):
-        rows = x[pl.ds(i * 16, 16), :].astype(f32)
-        normed = norm_rows(rows, g_row, s_row).astype(bf16)
-        for j in range(KCH):
-            u[j, pl.ds(i * 16, 16), :] = normed[:, j * KCS:(j + 1) * KCS]
-    acc[...] = jnp.broadcast_to(b_qkv[layer:layer + 1, :].astype(f32), (NB, QW))
+        g_row = gain[layer, 0:1, :].astype(f32)
+        s_row = shift[layer, 0:1, :].astype(f32)
+        for i in range(NB // 16):
+            rows = x[pl.ds(i * 16, 16), :].astype(f32)
+            normed = norm_rows(rows, g_row, s_row).astype(bf16)
+            for j in range(KCH):
+                u[j, pl.ds(i * 16, 16), :] = normed[:, j * KCS:(j + 1) * KCS]
+        acc[...] = jnp.broadcast_to(b_qkv[layer:layer + 1, :].astype(f32), (NB, QW))
+    else:
+        fetch_cache()
     qs[...] = jnp.zeros_like(qs)
-
     cos_t, sin_t = rope_tables(pos)
-
-    def qkv_step(i, carry):
-        w_copy(i).wait()
-        acc[...] += jnp.dot(u[i], w[i], preferred_element_type=f32)
-        return carry
-
-    lax.fori_loop(0, KCH, qkv_step, 0)
+    if layer == 0:
+        def qkv_step(i, carry):
+            w_copy(i).wait()
+            acc[...] += jnp.dot(u[i], w[i], preferred_element_type=f32)
+            return carry
+
+        lax.fori_loop(0, KCH, qkv_step, 0)
 
     for c in range(KVL):
         for j in range(GRP + 2):
-            col = (c * (GRP + 2) + j) * HD
-            tile = acc[:, col:col + HD]
+            if layer == 0:
+                col = (c * (GRP + 2) + j) * HD
+                tile = acc[:, col:col + HD]
+            else:
+                tile = acc[c, :, j * HD:(j + 1) * HD]
             if j <= GRP:
                 tile = tile * cos_t + pltpu.roll(tile, HD // 2, 1) * sin_t
             for i in range(NB // 8):
@@ -210,21 +219,28 @@
         out_copy(vbuf, vo_hbm, 1, i).wait()
 
 
-def attn_call(layer, pos, x, gain, shift, b_qkv, w_qkv, k_cache, v_cache, prev):
+def attn_call(layer, pos, operands, k_cache, v_cache, prev):
     vm = pl.BlockSpec(memory_space=pltpu.VMEM)
     hbm = pl.BlockSpec(memory_space=pltpu.HBM)
-    args = [pos, x, gain, shift, b_qkv, w_qkv, k_cache, v_cache]
+    args = [pos, *operands, k_cache, v_cache]
     if layer == 0:
         specs = [hbm] * 8
         alias = {}
-        small = [pltpu.SMEM(pos.shape, jnp.int32)] + [pltpu.VMEM(arr.shape, bf16) for arr in (x, gain, shift, b_qkv)]
-        small.append(pltpu.SemaphoreType.DMA((5,)))
+        extra = [
+            pltpu.VMEM((KCH, KCS, QW), bf16),
+            pltpu.VMEM((KCH, NB, KCS), bf16),
+            pltpu.VMEM((NB, QW), f32),
+            pltpu.SemaphoreType.DMA((KCH,)),
+            pltpu.SMEM(pos.shape, jnp.int32),
+            *[pltpu.VMEM(arr.shape, bf16) for arr in operands[:4]],
+            pltpu.SemaphoreType.DMA((5,)),
+        ]
         limit = 60 * 1024 * 1024
     else:
         args += list(prev)
-        specs = [pl.BlockSpec(memory_space=pltpu.SMEM)] + [vm] * 4 + [hbm] * 5
-        alias = {8: 1, 9: 2}
-        small = []
+        specs = [pl.BlockSpec(memory_space=pltpu.SMEM), vm] + [hbm] * 4
+        alias = {4: 1, 5: 2}
+        extra = []
         limit = VMEM_BYTES
     cache = jax.ShapeDtypeStruct(k_cache.shape, bf16)
     return pl.pallas_call(
@@ -233,22 +249,18 @@
         in_specs=specs,
         out_specs=(vm, hbm, hbm),
         scratch_shapes=[
-            pltpu.VMEM((KCH, KCS, QW), bf16),
             pltpu.VMEM((NB, SLOTS * KVL, HD), bf16),
             pltpu.VMEM((NB, SLOTS * KVL, HD), bf16),
-            pltpu.VMEM((KCH, NB, KCS), bf16),
-            pltpu.VMEM((NB, QW), f32),
             pltpu.VMEM((NB * QROWS, HD), f32),
             pltpu.VMEM((NB * 8, HD), f32),
             pltpu.VMEM((NB * 8, HD), f32),
             pltpu.VMEM((NB * QROWS, HD), f32),
             pltpu.VMEM((NB * QROWS, HD), f32),
             pltpu.VMEM((NB * QROWS, HD), f32),
-            pltpu.SemaphoreType.DMA((KCH,)),
             pltpu.SemaphoreType.DMA((NG,)),
             pltpu.SemaphoreType.DMA((NG,)),
             pltpu.SemaphoreType.DMA((2, NG)),
-            *small,
+            *extra,
         ],
         input_output_aliases=alias,
         compiler_params=pltpu.CompilerParams(vmem_limit_bytes=limit),
@@ -256,9 +268,13 @@
     )(*args)
 
 
-def rest_kernel(layer, msg, x, gain, shift, b_dense, b_up, b_down, wd_hbm, wu_hbm, wn_hbm, out,
-                wd, wu, wn, got, sent, o_buf, part, pair, sums, other, ag, full, xrow, up, mbuf,
-                wsem, a_sem, d_sem, y_sem, g_sem, x_sem):
+def rest_kernel(layer, msg, x, gain, shift, b_dense, b_up, b_down, wd_hbm, wu_hbm, wn_hbm, *rest):
+    if layer == 0:
+        b_qkv, wq_hbm, x_out, out, *rest = rest
+    else:
+        out, *rest = rest
+    (wd, wu, wn, got, sent, o_buf, part, pair, sums, other, ag, full, xrow, up, mbuf,
+     wsem, a_sem, d_sem, y_sem, g_sem, x_sem) = rest
     dp = lax.axis_index('dp')
     tp = lax.axis_index('tp')
     sp = lax.axis_index('sp')
@@ -279,6 +295,9 @@
 
     wn_copy = load(wn_hbm.at[layer, pl.ds(pl.multiple_of(core * M_LOC, M_LOC), M_LOC), :], wn, 1 + NCH)
 
+    def wq_copy(i):
+        return load(wq_hbm.at[1, pl.ds(i * CW, CW), :], wu.at[i, :, pl.ds(0, QW)], 2 + NCH + i)
+
     barrier = pltpu.get_barrier_semaphore()
     for peer in (mate, x_dev, y_dev):
         pl.semaphore_signal(barrier, inc=1, device_id=peer, device_id_type=MESH)
@@ -308,7 +327,7 @@
     def all_rows(x_, c_):
         return pl.ds(pl.multiple_of(x_ * HALF + c_ * ROWS, ROWS), ROWS)
 
-    xrow[...] = x[all_rows(cx, core), :].astype(f32)
+    xrow[...] = x[all_rows(cx, core), :].astype(f32) if layer == 0 else x[...]
     lane = lax.broadcasted_iota(jnp.int32, (8, HD), 1)
 
     def merge(one, two, put, stat_out=None):
@@ -390,6 +409,8 @@
         wu_copy(n).wait()
         swap[n].wait_recv()
         up[...] += jnp.dot(ag[n].astype(bf16), wu[n], preferred_element_type=f32)
+        if layer == 0:
+            wq_copy(n).start()
 
     pick = (lax.broadcasted_iota(jnp.int32, (256, 128), 0) == 2 * lax.broadcasted_iota(jnp.int32, (256, 128), 1))
     pick = jnp.where(pick, 1.0, 0.0).astype(bf16)
@@ -404,39 +425,72 @@
     m = mbuf[...]
     sends += swap
 
-    def spread(n, total):
-        residual(n, total, b_down)
-        full[n, all_rows(cx, core), :] = xrow[:, n * CW:(n + 1) * CW]
+    def spread(n, value):
+        full[n, all_rows(cx, core), :] = value
         here = full.at[n, all_rows(cx, core), :]
         for k, peer in enumerate((x_dev, mate)):
             copy = remote(here, here, x_sem, (k, n), peer)
             copy.start()
             sends.append(copy)
 
-    sends += reduce(1, lambda n: jnp.dot(m, wn[:, n * CW:(n + 1) * CW], preferred_element_type=f32), spread)
-    for n in range(NCH):
-        there = full.at[n, all_rows(ox, core), :]
-        remote(there, there, x_sem, (0, n), x_dev).wait_recv()
-        copy = remote(there, there, x_sem, (2, n), mate)
-        copy.start()
-        sends.append(copy)
-    for n in range(NCH):
-        for k, x_ in ((1, cx), (2, ox)):
-            there = full.at[n, all_rows(x_, 1 - core), :]
-            remote(there, there, x_sem, (k, n), mate).wait_recv()
-        out[:, n * CW:(n + 1) * CW] = full[n].astype(bf16)
+    def collect(use):
+        for n in range(NCH):
+            there = full.at[n, all_rows(ox, core), :]
+            remote(there, there, x_sem, (0, n), x_dev).wait_recv()
+            copy = remote(there, there, x_sem, (2, n), mate)
+            copy.start()
+            sends.append(copy)
+        for n in range(NCH):
+            for k, x_ in ((1, cx), (2, ox)):
+                there = full.at[n, all_rows(x_, 1 - core), :]
+                remote(there, there, x_sem, (k, n), mate).wait_recv()
+            use(n)
+
+    def take_down(n, total):
+        residual(n, total, b_down)
+        if layer == 1:
+            spread(n, xrow[:, n * CW:(n + 1) * CW])
+
+    sends += reduce(1, lambda n: jnp.dot(m, wn[:, n * CW:(n + 1) * CW], preferred_element_type=f32), take_down)
+    if layer == 0:
+        x_out[...] = xrow[...]
+        u = norm_rows(xrow[...], gain[1, 0:1, :].astype(f32), shift[1, 0:1, :].astype(f32)).astype(bf16)
+        for i in range(NCH):
+            wq_copy(i).wait()
+        for n in range(NCH):
+            cols = slice(n * QC, (n + 1) * QC)
+            r = jnp.broadcast_to(b_qkv[1:2, cols].astype(f32), (ROWS, QC))
+            for i in range(NCH):
+                r += jnp.dot(u[:, i * CW:(i + 1) * CW], wu[i, :, cols], preferred_element_type=f32)
+            spread(n, r)
+
+        def use(n):
+            out[n] = full[n]
+    else:
+        def use(n):
+            out[:, n * CW:(n + 1) * CW] = full[n].astype(bf16)
+
+    collect(use)
     for copy in sends:
         copy.wait_send()
 
 
-def rest_call(layer, msg, x, gain, shift, b_dense, b_up, b_down, w_dense, w_up, w_down):
+def rest_call(layer, msg, x, gain, shift, b_dense, b_up, b_down, w_dense, w_up, w_down, *qkv):
     vm = pl.BlockSpec(memory_space=pltpu.VMEM)
     hbm = pl.BlockSpec(memory_space=pltpu.HBM)
+    if layer == 0:
+        in_specs = [vm] * 7 + [hbm] * 3 + [vm, hbm]
+        out_shape = (jax.ShapeDtypeStruct((ROWS, D), f32), jax.ShapeDtypeStruct((NCH, NB, QC), f32))
+        out_specs = (vm, vm)
+    else:
+        in_specs = [vm] * 7 + [hbm] * 3
+        out_shape = jax.ShapeDtypeStruct((NB, D), bf16)
+        out_specs = vm
     return pl.pallas_call(
         functools.partial(rest_kernel, layer),
-        out_shape=jax.ShapeDtypeStruct((NB, D), bf16),
-        in_specs=[vm] * 7 + [hbm] * 3,
-        out_specs=vm,
+        out_shape=out_shape,
+        in_specs=in_specs,
+        out_specs=out_specs,
         scratch_shapes=[
             pltpu.VMEM((DR, D), bf16),
             pltpu.VMEM((NCH, CW, F_LOC), bf16),
@@ -449,11 +503,11 @@
             pltpu.VMEM((2, NCH, ROWS, CW), f32),
             pltpu.VMEM((2, NCH, ROWS, CW), f32),
             pltpu.VMEM((NCH, HALF, CW), f32),
-            pltpu.VMEM((NCH, NB, CW), f32),
+            pltpu.VMEM((NCH, NB, QC if layer == 0 else CW), f32),
             pltpu.VMEM((ROWS, D), f32),
             pltpu.VMEM((HALF, F_LOC), f32),
             pltpu.VMEM((HALF, M_LOC), bf16),
-            pltpu.SemaphoreType.DMA((2 + NCH,)),
+            pltpu.SemaphoreType.DMA((2 + 2 * NCH,)),
             pltpu.SemaphoreType.DMA((2, 3)),
             pltpu.SemaphoreType.DMA((2, 2, NCH)),
             pltpu.SemaphoreType.DMA((2, 2, NCH)),
@@ -462,7 +516,7 @@
         ],
         compiler_params=pltpu.CompilerParams(vmem_limit_bytes=VMEM_BYTES, collective_id=layer, has_side_effects=True),
         name=f'rest{layer}',
-    )(msg, x, gain, shift, b_dense, b_up, b_down, w_dense, w_up, w_down)
+    )(msg, x, gain, shift, b_dense, b_up, b_down, w_dense, w_up, w_down, *qkv)
 
 
 def solution(mesh):
@@ -475,10 +529,11 @@
         flat = (2, NB, SLOTS * KVL, HD)
         k_cache = k_cache.reshape(flat)
         v_cache = v_cache.reshape(flat)
-        caches = None
-        for layer in range(2):
-            msg, *caches = attn_call(layer, positions, hidden, ln_gain, ln_bias, b_qkv, w_qkv, k_cache, v_cache, caches)
-            hidden = rest_call(layer, msg, hidden, ln_gain, ln_bias, b_dense, b_up, b_down, w_dense, w_up, w_down)
+        shared = (ln_gain, ln_bias, b_dense, b_up, b_down, w_dense, w_up, w_down)
+        msg, *caches = attn_call(0, positions, (hidden, ln_gain, ln_bias, b_qkv, w_qkv), k_cache, v_cache, None)
+        rows, qkv = rest_call(0, msg, hidden, *shared, b_qkv, w_qkv)
+        msg, *caches = attn_call(1, positions, (qkv,), k_cache, v_cache, caches)
+        hidden = rest_call(1, msg, rows, *shared)
         return hidden, caches[0].reshape(shape), caches[1].reshape(shape)
 
     return jax.shard_map(device_step, mesh=mesh, in_specs=in_specs, out_specs=out_specs, check_vma=False)

time: 103 us -> 99.7 us (0.968)
  Pallas kernels: 99.9 us -> 97 us
    pallas_call x2, Pallas kernels: 30.2 us -> 23.8 us  [attn_call(): pl.pallas_call(functools.partial(attn_kernel, layer), out_shape=(jax.Shap...]
    pallas_call x2, Pallas kernels: 69.7 us -> 73.2 us  [rest_call(): pl.pallas_call(functools.partial(rest_kernel, layer), out_shape=out_shape...]
where the time goes in v1:
time: 99.7 us; the launch traced here: 99.5 us
  Pallas kernels  97 us (97%)
  local copies, waits for them, and re-layouts  1.78 us (2%)
    pallas_call x2, Pallas kernels, rest_call(): pl.pallas_call(functools.partial(rest_kernel, layer), out_shape=out_shape...  73.2 us
    pallas_call x2, Pallas kernels, attn_call(): pl.pallas_call(functools.partial(attn_kernel, layer), out_shape=(jax.Shap...  23.8 us

profile of v1, /device:TPU:0, one launch (start us, length us, event | category | flops | bytes accessed | tf_op | source)
XLA Modules:
  0.0 99.5 jit_solution(17807282419256976508)
XLA Ops:
  0.6 0.0 copy-start
  0.6 0.0 copy-start.2
  0.7 0.0 copy-start.3
  0.7 0.0 copy-start.4
  0.7 0.0 copy-start.5
  0.7 0.0 copy-start.6
  0.7 0.0 copy-start.7
  0.7 15.4 %attn0.1 = (f32[4,200,128]{2,1,0:T(8,128)}, bf16[2,64,256,128]{3,2,1,0:T(8,128)(2,1)}, bf16[2,64,256,128]{3,2,1,0:T(8,128)(2,1)}) custom-call(s32[64]{0:T(128)} %pos.3, bf16[64,3072]{1,0:T(8,128)(2,1)} %x.1, bf16[2,2,3072]{2,1,0:T(2,128)(2,1)} %gain.3, bf16[2,2,3072]{2,1,0:T(2,128)(2,1)} %shift.3, bf16[2,2560]{1,0:T(2,128)(2,1)} %rest_0_.3, ...), custom_call_target="tpu_custom_call" | custom-call | tf_op jit(solution)/shard_map/attn0/pallas_call | solution.py:246
  16.2 0.0 copy-done
  16.2 0.0 copy-done.2
  16.2 0.0 copy-done.3
  16.2 0.0 copy-done.4
  16.2 0.0 copy-done.5
  16.2 0.0 copy-done.6
  16.2 0.0 copy-done.7
  16.2 0.0 copy-start.1
  16.2 1.0 copy-done.1
  17.2 0.0 copy-start.8
  17.2 38.9 %rest0.1 = (f32[16,3072]{1,0:T(8,128)S(1)}, f32[4,64,640]{2,1,0:T(8,128)S(1)}) custom-call(f32[4,200,128]{2,1,0:T(8,128)S(1)} %copy-done.1, bf16[64,3072]{1,0:T(8,128)(2,1)S(1)} %copy-done, bf16[2,2,3072]{2,1,0:T(2,128)(2,1)S(1)} %copy-done.2, bf16[2,2,3072]{2,1,0:T(2,128)(2,1)S(1)} %copy-done.3, bf16[2,3072]{1,0:T(2,128)(2,1)S(1)} %copy-done.5, ...), custom_call_target="tpu_custom_call" | custom-call | tf_op jit(solution)/shard_map/rest0/pallas_call | solution.py:489
  56.1 0.0 copy-done.8
  56.1 8.3 %attn1.1 = (f32[4,200,128]{2,1,0:T(8,128)S(1)}, bf16[2,64,256,128]{3,2,1,0:T(8,128)(2,1)}, bf16[2,64,256,128]{3,2,1,0:T(8,128)(2,1)}) custom-call(s32[64]{0:T(128)S(1)} %copy-done.8, f32[4,64,640]{2,1,0:T(8,128)S(1)} %get-tuple-element.12.rest_0_, bf16[2,64,256,128]{3,2,1,0:T(8,128)(2,1)} %bitcast.5, ...), custom_call_target="tpu_custom_call", output_to_operand_aliasing={{1}: (4, {}), {2}: (5, {})} | custom-call | tf_op jit(solution)/shard_map/attn1/pallas_call | solution.py:246
  64.5 34.3 %rest1.1 = bf16[64,3072]{1,0:T(8,128)(2,1)S(1)} custom-call(f32[4,200,128]{2,1,0:T(8,128)S(1)} %get-tuple-element.15.msg, f32[16,3072]{1,0:T(8,128)S(1)} %get-tuple-element.16.x, bf16[2,2,3072]{2,1,0:T(2,128)(2,1)S(1)} %copy-done.2, bf16[2,2,3072]{2,1,0:T(2,128)(2,1)S(1)} %copy-done.3, bf16[2,3072]{1,0:T(2,128)(2,1)S(1)} %copy-done.5, ...), custom_call_target="tpu_custom_call" | custom-call | tf_op jit(solution)/shard_map/rest1/pallas_call | solution.py:489
  98.8 0.7 copy.22
Async XLA Ops:
  0.6 15.5 %copy-start = (bf16[64,3072]{1,0:T(8,128)(2,1)S(1)}, bf16[64,3072]{1,0:T(8,128)(2,1)}, u32[]{:S(2)}) copy-start(bf16[64,3072]{1,0:T(8,128)(2,1)} %x.1) | copy-start | bytes 1179652
  0.6 15.5 %copy-start.2 = (bf16[2,2,3072]{2,1,0:T(2,128)(2,1)S(1)}, bf16[2,2,3072]{2,1,0:T(2,128)(2,1)}, u32[]{:S(2)}) copy-start(bf16[2,2,3072]{2,1,0:T(2,128)(2,1)} %gain.3) | copy-start | bytes 73732
  0.7 15.5 %copy-start.3 = (bf16[2,2,3072]{2,1,0:T(2,128)(2,1)S(1)}, bf16[2,2,3072]{2,1,0:T(2,128)(2,1)}, u32[]{:S(2)}) copy-start(bf16[2,2,3072]{2,1,0:T(2,128)(2,1)} %shift.3) | copy-start | bytes 73732
  0.7 15.5 %copy-start.4 = (bf16[2,8192]{1,0:T(2,128)(2,1)S(1)}, bf16[2,8192]{1,0:T(2,128)(2,1)}, u32[]{:S(2)}) copy-start(bf16[2,8192]{1,0:T(2,128)(2,1)} %b_up.3) | copy-start | bytes 98308
  0.7 15.5 %copy-start.5 = (bf16[2,3072]{1,0:T(2,128)(2,1)S(1)}, bf16[2,3072]{1,0:T(2,128)(2,1)}, u32[]{:S(2)}) copy-start(bf16[2,3072]{1,0:T(2,128)(2,1)} %b_dense.3) | copy-start | bytes 36868
  0.7 15.5 %copy-start.6 = (bf16[2,3072]{1,0:T(2,128)(2,1)S(1)}, bf16[2,3072]{1,0:T(2,128)(2,1)}, u32[]{:S(2)}) copy-start(bf16[2,3072]{1,0:T(2,128)(2,1)} %b_down.3) | copy-start | bytes 36868
  0.7 15.5 %copy-start.7 = (bf16[2,2560]{1,0:T(2,128)(2,1)S(1)}, bf16[2,2560]{1,0:T(2,128)(2,1)}, u32[]{:S(2)}) copy-start(bf16[2,2560]{1,0:T(2,128)(2,1)} %rest_0_.3) | copy-start | bytes 30724
  16.2 1.0 %copy-start.1 = (f32[4,200,128]{2,1,0:T(8,128)S(1)}, f32[4,200,128]{2,1,0:T(8,128)}, u32[]{:S(2)}) copy-start(f32[4,200,128]{2,1,0:T(8,128)} %get-tuple-element.11.msg) | copy-start | bytes 1228804
  17.2 38.9 %copy-start.8 = (s32[64]{0:T(128)S(1)}, s32[64]{0:T(128)}, u32[]{:S(2)}) copy-start(s32[64]{0:T(128)} %pos.3) | copy-start | bytes 772

commit v2 on v1

--- a/solution.py
+++ b/solution.py
@@ -35,9 +35,10 @@
 ROWS = HALF // 2
 F_LOC = 4096
 M_LOC = F_LOC // 2
-NCH = 4
+NCH = 6
 CW = D // NCH
-QC = QW // NCH
+QCH = 4
+QC = QW // QCH
 DR = HPC * HD
 LAG = 2
 VMEM_BYTES = 52 * 1024 * 1024
@@ -191,11 +192,8 @@
             ls[rows, :] = jnp.broadcast_to(sums[bi], (QROWS, HD))
             os[rows, :] = outs[bi]
 
-        @pl.when(i > 0)
-        def _():
-            out_copy(kbuf, ko_hbm, 0, i - 1).start()
-            out_copy(vbuf, vo_hbm, 1, i - 1).start(priority=1)
-
+        out_copy(kbuf, ko_hbm, 0, i).start()
+        out_copy(vbuf, vo_hbm, 1, i).start(priority=1)
         return carry
 
     lax.fori_loop(0, NG, attn_step, 0)
@@ -212,8 +210,6 @@
                     stat = jnp.where(lane == at, ms[rows, :], stat)
                     stat = jnp.where(lane == at + 1, ls[rows, :], stat)
             msg[half * 2 + c, pl.ds(HPC * HALF, 8), :] = stat
-    out_copy(kbuf, ko_hbm, 0, NG - 1).start()
-    out_copy(vbuf, vo_hbm, 1, NG - 1).start(priority=1)
     for i in range(NG):
         out_copy(kbuf, ko_hbm, 0, i).wait()
         out_copy(vbuf, vo_hbm, 1, i).wait()
@@ -366,8 +362,7 @@
     merge(msg.at[near], got.at[1], put_part(sent.at[1]), sent.at[1])
     cross.wait_recv()
     merge(sent.at[1], got.at[2], put_out)
-    for copy in swap + [cross]:
-        copy.wait_send()
+    sends = swap + [cross]
 
     def reduce(ph, product, finish):
         first = [remote(part.at[ph, n, theirs, :], pair.at[ph, n], d_sem, (ph, n), mate) for n in range(NCH)]
@@ -393,7 +388,7 @@
 
     wd_copy.wait()
     o = o_buf[...].astype(bf16)
-    sends = reduce(0, lambda n: jnp.dot(o, wd[:, n * CW:(n + 1) * CW], preferred_element_type=f32),
+    sends += reduce(0, lambda n: jnp.dot(o, wd[:, n * CW:(n + 1) * CW], preferred_element_type=f32),
                    lambda n, total: residual(n, total, b_dense))
 
     normed = norm_rows(xrow[...], gain1, shift1).astype(bf16).astype(f32)
@@ -433,14 +428,14 @@
             copy.start()
             sends.append(copy)
 
-    def collect(use):
-        for n in range(NCH):
+    def collect(chunks, use):
+        for n in range(chunks):
             there = full.at[n, all_rows(ox, core), :]
             remote(there, there, x_sem, (0, n), x_dev).wait_recv()
             copy = remote(there, there, x_sem, (2, n), mate)
             copy.start()
             sends.append(copy)
-        for n in range(NCH):
+        for n in range(chunks):
             for k, x_ in ((1, cx), (2, ox)):
                 there = full.at[n, all_rows(x_, 1 - core), :]
                 remote(there, there, x_sem, (k, n), mate).wait_recv()
@@ -457,7 +452,7 @@
         u = norm_rows(xrow[...], gain[1, 0:1, :].astype(f32), shift[1, 0:1, :].astype(f32)).astype(bf16)
         for i in range(NCH):
             wq_copy(i).wait()
-        for n in range(NCH):
+        for n in range(QCH):
             cols = slice(n * QC, (n + 1) * QC)
             r = jnp.broadcast_to(b_qkv[1:2, cols].astype(f32), (ROWS, QC))
             for i in range(NCH):
@@ -470,7 +465,7 @@
         def use(n):
             out[:, n * CW:(n + 1) * CW] = full[n].astype(bf16)
 
-    collect(use)
+    collect(QCH if layer == 0 else NCH, use)
     for copy in sends:
         copy.wait_send()
 
@@ -480,7 +475,7 @@
     hbm = pl.BlockSpec(memory_space=pltpu.HBM)
     if layer == 0:
         in_specs = [vm] * 7 + [hbm] * 3 + [vm, hbm]
-        out_shape = (jax.ShapeDtypeStruct((ROWS, D), f32), jax.ShapeDtypeStruct((NCH, NB, QC), f32))
+        out_shape = (jax.ShapeDtypeStruct((ROWS, D), f32), jax.ShapeDtypeStruct((QCH, NB, QC), f32))
         out_specs = (vm, vm)
     else:
         in_specs = [vm] * 7 + [hbm] * 3
@@ -503,7 +498,7 @@
             pltpu.VMEM((2, NCH, ROWS, CW), f32),
             pltpu.VMEM((2, NCH, ROWS, CW), f32),
             pltpu.VMEM((NCH, HALF, CW), f32),
-            pltpu.VMEM((NCH, NB, QC if layer == 0 else CW), f32),
+            pltpu.VMEM((QCH, NB, QC) if layer == 0 else (NCH, NB, CW), f32),
             pltpu.VMEM((ROWS, D), f32),
             pltpu.VMEM((HALF, F_LOC), f32),
             pltpu.VMEM((HALF, M_LOC), bf16),

time: 99.7 us -> 97.2 us (0.975)
  Pallas kernels: 97 us -> 94.5 us
    pallas_call x2, Pallas kernels: 73.2 us -> 71.3 us  [rest_call(): pl.pallas_call(functools.partial(rest_kernel, layer), out_shape=out_shape...]
where the time goes in v2:
time: 97.2 us; the launch traced here: 97 us
  Pallas kernels  94.5 us (97%)
  local copies, waits for them, and re-layouts  1.78 us (2%)
    pallas_call x2, Pallas kernels, rest_call(): pl.pallas_call(functools.partial(rest_kernel, layer), out_shape=out_shape...  71.3 us
    pallas_call x2, Pallas kernels, attn_call(): pl.pallas_call(functools.partial(attn_kernel, layer), out_shape=(jax.Shap...  23.1 us

profile of v2, /device:TPU:0, one launch (start us, length us, event | category | flops | bytes accessed | tf_op | source)
XLA Modules:
  0.0 97.0 jit_solution(8221064002544844246)
XLA Ops:
  0.6 0.0 copy-start
  0.6 0.0 copy-start.2
  0.7 0.0 copy-start.3
  0.7 0.0 copy-start.4
  0.7 0.0 copy-start.5
  0.7 0.0 copy-start.6
  0.7 0.0 copy-start.7
  0.7 15.2 %attn0.1 = (f32[4,200,128]{2,1,0:T(8,128)}, bf16[2,64,256,128]{3,2,1,0:T(8,128)(2,1)}, bf16[2,64,256,128]{3,2,1,0:T(8,128)(2,1)}) custom-call(s32[64]{0:T(128)} %pos.3, bf16[64,3072]{1,0:T(8,128)(2,1)} %x.1, bf16[2,2,3072]{2,1,0:T(2,128)(2,1)} %gain.3, bf16[2,2,3072]{2,1,0:T(2,128)(2,1)} %shift.3, bf16[2,2560]{1,0:T(2,128)(2,1)} %rest_0_.3, ...), custom_call_target="tpu_custom_call" | custom-call | tf_op jit(solution)/shard_map/attn0/pallas_call | solution.py:242
  15.9 0.0 copy-done
  15.9 0.0 copy-done.2
  15.9 0.0 copy-done.3
  15.9 0.0 copy-done.4
  15.9 0.0 copy-done.5
  15.9 0.0 copy-done.6
  15.9 0.0 copy-done.7
  16.0 0.0 copy-start.1
  16.0 1.0 %copy-done.1 = f32[4,200,128]{2,1,0:T(8,128)S(1)} copy-done((f32[4,200,128]{2,1,0:T(8,128)S(1)}, f32[4,200,128]{2,1,0:T(8,128)}, u32[]{:S(2)}) %copy-start.1) | copy-done | bytes 409624
  17.0 0.0 copy-start.8
  17.0 38.0 %rest0.1 = (f32[16,3072]{1,0:T(8,128)S(1)}, f32[4,64,640]{2,1,0:T(8,128)S(1)}) custom-call(f32[4,200,128]{2,1,0:T(8,128)S(1)} %copy-done.1, bf16[64,3072]{1,0:T(8,128)(2,1)S(1)} %copy-done, bf16[2,2,3072]{2,1,0:T(2,128)(2,1)S(1)} %copy-done.2, bf16[2,2,3072]{2,1,0:T(2,128)(2,1)S(1)} %copy-done.3, bf16[2,3072]{1,0:T(2,128)(2,1)S(1)} %copy-done.5, ...), custom_call_target="tpu_custom_call" | custom-call | tf_op jit(solution)/shard_map/rest0/pallas_call | solution.py:484
  55.0 0.0 copy-done.8
  55.0 7.9 %attn1.1 = (f32[4,200,128]{2,1,0:T(8,128)S(1)}, bf16[2,64,256,128]{3,2,1,0:T(8,128)(2,1)}, bf16[2,64,256,128]{3,2,1,0:T(8,128)(2,1)}) custom-call(s32[64]{0:T(128)S(1)} %copy-done.8, f32[4,64,640]{2,1,0:T(8,128)S(1)} %get-tuple-element.12.rest_0_, bf16[2,64,256,128]{3,2,1,0:T(8,128)(2,1)} %bitcast.5, ...), custom_call_target="tpu_custom_call", output_to_operand_aliasing={{1}: (4, {}), {2}: (5, {})} | custom-call | tf_op jit(solution)/shard_map/attn1/pallas_call | solution.py:242
  62.9 33.4 %rest1.1 = bf16[64,3072]{1,0:T(8,128)(2,1)S(1)} custom-call(f32[4,200,128]{2,1,0:T(8,128)S(1)} %get-tuple-element.15.msg, f32[16,3072]{1,0:T(8,128)S(1)} %get-tuple-element.16.x, bf16[2,2,3072]{2,1,0:T(2,128)(2,1)S(1)} %copy-done.2, bf16[2,2,3072]{2,1,0:T(2,128)(2,1)S(1)} %copy-done.3, bf16[2,3072]{1,0:T(2,128)(2,1)S(1)} %copy-done.5, ...), custom_call_target="tpu_custom_call" | custom-call | tf_op jit(solution)/shard_map/rest1/pallas_call | solution.py:484
  96.3 0.7 copy.22
Async XLA Ops:
  0.6 15.3 %copy-start = (bf16[64,3072]{1,0:T(8,128)(2,1)S(1)}, bf16[64,3072]{1,0:T(8,128)(2,1)}, u32[]{:S(2)}) copy-start(bf16[64,3072]{1,0:T(8,128)(2,1)} %x.1) | copy-start | bytes 1179652
  0.6 15.3 %copy-start.2 = (bf16[2,2,3072]{2,1,0:T(2,128)(2,1)S(1)}, bf16[2,2,3072]{2,1,0:T(2,128)(2,1)}, u32[]{:S(2)}) copy-start(bf16[2,2,3072]{2,1,0:T(2,128)(2,1)} %gain.3) | copy-start | bytes 73732
  0.7 15.3 %copy-start.3 = (bf16[2,2,3072]{2,1,0:T(2,128)(2,1)S(1)}, bf16[2,2,3072]{2,1,0:T(2,128)(2,1)}, u32[]{:S(2)}) copy-start(bf16[2,2,3072]{2,1,0:T(2,128)(2,1)} %shift.3) | copy-start | bytes 73732
  0.7 15.3 %copy-start.4 = (bf16[2,8192]{1,0:T(2,128)(2,1)S(1)}, bf16[2,8192]{1,0:T(2,128)(2,1)}, u32[]{:S(2)}) copy-start(bf16[2,8192]{1,0:T(2,128)(2,1)} %b_up.3) | copy-start | bytes 98308
  0.7 15.3 %copy-start.5 = (bf16[2,3072]{1,0:T(2,128)(2,1)S(1)}, bf16[2,3072]{1,0:T(2,128)(2,1)}, u32[]{:S(2)}) copy-start(bf16[2,3072]{1,0:T(2,128)(2,1)} %b_dense.3) | copy-start | bytes 36868
  0.7 15.3 %copy-start.6 = (bf16[2,3072]{1,0:T(2,128)(2,1)S(1)}, bf16[2,3072]{1,0:T(2,128)(2,1)}, u32[]{:S(2)}) copy-start(bf16[2,3072]{1,0:T(2,128)(2,1)} %b_down.3) | copy-start | bytes 36868
  0.7 15.3 %copy-start.7 = (bf16[2,2560]{1,0:T(2,128)(2,1)S(1)}, bf16[2,2560]{1,0:T(2,128)(2,1)}, u32[]{:S(2)}) copy-start(bf16[2,2560]{1,0:T(2,128)(2,1)} %rest_0_.3) | copy-start | bytes 30724
  16.0 1.0 %copy-start.1 = (f32[4,200,128]{2,1,0:T(8,128)S(1)}, f32[4,200,128]{2,1,0:T(8,128)}, u32[]{:S(2)}) copy-start(f32[4,200,128]{2,1,0:T(8,128)} %get-tuple-element.11.msg) | copy-start | bytes 1228804
  17.0 38.0 %copy-start.8 = (s32[64]{0:T(128)S(1)}, s32[64]{0:T(128)}, u32[]{:S(2)}) copy-start(s32[64]{0:T(128)} %pos.3) | copy-start | bytes 772

commit v3 on v2

--- a/solution.py
+++ b/solution.py
@@ -29,6 +29,7 @@
 KCS = D // KCH
 G = 8
 NG = NB // G
+GS = 16
 HALF = NB // 2
 HPC = 6
 MSG = HPC * HALF + 8
@@ -40,7 +41,9 @@
 QCH = 4
 QC = QW // QCH
 DR = HPC * HD
-LAG = 2
+RCH = 12
+RW = D // RCH
+LAG = 5
 VMEM_BYTES = 52 * 1024 * 1024
 
 f32 = jnp.float32
@@ -153,11 +156,13 @@
     sub_row = lax.broadcasted_iota(jnp.int32, (16, HD), 0) // KVL
 
     def attn_step(i, carry):
-        in_copy(kc_hbm, kbuf, ksem, i).wait()
-        in_copy(vc_hbm, vbuf, vsem, i).wait()
+        copies = [i * (GS // G) + j for j in range(GS // G)]
+        for j in copies:
+            in_copy(kc_hbm, kbuf, ksem, j).wait()
+            in_copy(vc_hbm, vbuf, vsem, j).wait()
         limits = []
-        for bi in range(G):
-            b = i * G + bi
+        for bi in range(GS):
+            b = i * GS + bi
             p = pos[b]
             pl_ = p - base
             pc = jnp.clip(pl_, 0, SLOTS - 1)
@@ -176,27 +181,28 @@
             else:
                 limits.append(pl_)
         scores = []
-        for bi in range(G):
-            b = i * G + bi
+        for bi in range(GS):
+            b = i * GS + bi
             q = qs[pl.ds(pl.multiple_of(b * QROWS, QROWS), QROWS), :].astype(bf16)
             scores.append(lax.dot_general(q, kbuf[b], (((1,), (1,)), ((), ())), preferred_element_type=f32))
         keeps = [slot_of <= limit for limit in limits]
         scores = [jnp.where(keep, s * (1.0 / HD), MASKED) for keep, s in zip(keeps, scores)]
         peaks = [jnp.max(s, axis=1, keepdims=True) for s in scores]
         weights = [jnp.where(keep, jnp.exp(s - peak), 0.0) for keep, s, peak in zip(keeps, scores, peaks)]
-        outs = [jnp.dot(wt.astype(bf16), vbuf[i * G + bi], preferred_element_type=f32) for bi, wt in enumerate(weights)]
+        outs = [jnp.dot(wt.astype(bf16), vbuf[i * GS + bi], preferred_element_type=f32) for bi, wt in enumerate(weights)]
         sums = [jnp.sum(wt, axis=1, keepdims=True) for wt in weights]
-        for bi in range(G):
-            rows = pl.ds(pl.multiple_of((i * G + bi) * QROWS, QROWS), QROWS)
+        for bi in range(GS):
+            rows = pl.ds(pl.multiple_of((i * GS + bi) * QROWS, QROWS), QROWS)
             ms[rows, :] = jnp.broadcast_to(peaks[bi], (QROWS, HD))
             ls[rows, :] = jnp.broadcast_to(sums[bi], (QROWS, HD))
             os[rows, :] = outs[bi]
 
-        out_copy(kbuf, ko_hbm, 0, i).start()
-        out_copy(vbuf, vo_hbm, 1, i).start(priority=1)
+        for j in copies:
+            out_copy(kbuf, ko_hbm, 0, j).start()
+            out_copy(vbuf, vo_hbm, 1, j).start(priority=1)
         return carry
 
-    lax.fori_loop(0, NG, attn_step, 0)
+    lax.fori_loop(0, NB // GS, attn_step, 0)
 
     lane = lax.broadcasted_iota(jnp.int32, (8, HD), 1)
     for half in range(2):
@@ -365,10 +371,10 @@
     sends = swap + [cross]
 
     def reduce(ph, product, finish):
-        first = [remote(part.at[ph, n, theirs, :], pair.at[ph, n], d_sem, (ph, n), mate) for n in range(NCH)]
-        second = [remote(sums.at[ph, n], other.at[ph, n], y_sem, (ph, n), y_dev) for n in range(NCH)]
-        for step in range(NCH + LAG):
-            if step < NCH:
+        first = [remote(part.at[ph, n, theirs, :], pair.at[ph, n], d_sem, (ph, n), mate) for n in range(RCH)]
+        second = [remote(sums.at[ph, n], other.at[ph, n], y_sem, (ph, n), y_dev) for n in range(RCH)]
+        for step in range(RCH + LAG):
+            if step < RCH:
                 part[ph, step] = product(step)
                 first[step].start()
             if step >= LAG:
@@ -376,19 +382,19 @@
                 first[n].wait_recv()
                 sums[ph, n] = part[ph, n, own, :] + pair[ph, n]
                 second[n].start()
-        for n in range(NCH):
+        for n in range(RCH):
             second[n].wait_recv()
             finish(n, sums[ph, n] + other[ph, n])
         return first + second
 
     def residual(n, total, bias):
-        cols = slice(n * CW, (n + 1) * CW)
+        cols = slice(n * RW, (n + 1) * RW)
         v = xrow[:, cols] + total + bias[layer:layer + 1, cols].astype(f32)
         xrow[:, cols] = v.astype(bf16).astype(f32)
 
     wd_copy.wait()
     o = o_buf[...].astype(bf16)
-    sends += reduce(0, lambda n: jnp.dot(o, wd[:, n * CW:(n + 1) * CW], preferred_element_type=f32),
+    sends += reduce(0, lambda n: jnp.dot(o, wd[:, n * RW:(n + 1) * RW], preferred_element_type=f32),
                    lambda n, total: residual(n, total, b_dense))
 
     normed = norm_rows(xrow[...], gain1, shift1).astype(bf16).astype(f32)
@@ -444,9 +450,9 @@
     def take_down(n, total):
         residual(n, total, b_down)
         if layer == 1:
-            spread(n, xrow[:, n * CW:(n + 1) * CW])
-
-    sends += reduce(1, lambda n: jnp.dot(m, wn[:, n * CW:(n + 1) * CW], preferred_element_type=f32), take_down)
+            spread(n, xrow[:, n * RW:(n + 1) * RW])
+
+    sends += reduce(1, lambda n: jnp.dot(m, wn[:, n * RW:(n + 1) * RW], preferred_element_type=f32), take_down)
     if layer == 0:
         x_out[...] = xrow[...]
         u = norm_rows(xrow[...], gain[1, 0:1, :].astype(f32), shift[1, 0:1, :].astype(f32)).astype(bf16)
@@ -463,9 +469,9 @@
             out[n] = full[n]
     else:
         def use(n):
-            out[:, n * CW:(n + 1) * CW] = full[n].astype(bf16)
-
-    collect(QCH if layer == 0 else NCH, use)
+            out[:, n * RW:(n + 1) * RW] = full[n].astype(bf16)
+
+    collect(QCH if layer == 0 else RCH, use)
     for copy in sends:
         copy.wait_send()
 
@@ -493,21 +499,21 @@
             pltpu.VMEM((3, MSG, HD), f32),
             pltpu.VMEM((2, MSG, HD), f32),
             pltpu.VMEM((HALF, DR), f32),
-            pltpu.VMEM((2, NCH, HALF, CW), f32),
-            pltpu.VMEM((2, NCH, ROWS, CW), f32),
-            pltpu.VMEM((2, NCH, ROWS, CW), f32),
-            pltpu.VMEM((2, NCH, ROWS, CW), f32),
+            pltpu.VMEM((2, RCH, HALF, RW), f32),
+            pltpu.VMEM((2, RCH, ROWS, RW), f32),
+            pltpu.VMEM((2, RCH, ROWS, RW), f32),
+            pltpu.VMEM((2, RCH, ROWS, RW), f32),
             pltpu.VMEM((NCH, HALF, CW), f32),
-            pltpu.VMEM((QCH, NB, QC) if layer == 0 else (NCH, NB, CW), f32),
+            pltpu.VMEM((QCH, NB, QC) if layer == 0 else (RCH, NB, RW), f32),
             pltpu.VMEM((ROWS, D), f32),
             pltpu.VMEM((HALF, F_LOC), f32),
             pltpu.VMEM((HALF, M_LOC), bf16),
             pltpu.SemaphoreType.DMA((2 + 2 * NCH,)),
             pltpu.SemaphoreType.DMA((2, 3)),
-            pltpu.SemaphoreType.DMA((2, 2, NCH)),
-            pltpu.SemaphoreType.DMA((2, 2, NCH)),
+            pltpu.SemaphoreType.DMA((2, 2, RCH)),
+            pltpu.SemaphoreType.DMA((2, 2, RCH)),
             pltpu.SemaphoreType.DMA((2, NCH)),
-            pltpu.SemaphoreType.DMA((2, 3, NCH)),
+            pltpu.SemaphoreType.DMA((2, 3, RCH)),
         ],
         compiler_params=pltpu.CompilerParams(vmem_limit_bytes=VMEM_BYTES, collective_id=layer, has_side_effects=True),
         name=f'rest{layer}',

time: 97.2 us -> 99 us (1.019)
  Pallas kernels: 94.5 us -> 96.3 us
    pallas_call x2, Pallas kernels: 71.3 us -> 74.9 us  [rest_call(): pl.pallas_call(functools.partial(rest_kernel, layer), out_shape=out_shape...]
    pallas_call x2, Pallas kernels: 23.1 us -> 21.5 us  [attn_call(): pl.pallas_call(functools.partial(attn_kernel, layer), out_shape=(jax.Shap...]
where the time goes in v3:
time: 99 us; the launch traced here: 98.9 us
  Pallas kernels  96.3 us (97%)
  local copies, waits for them, and re-layouts  1.78 us (2%)
    pallas_call x2, Pallas kernels, rest_call(): pl.pallas_call(functools.partial(rest_kernel, layer), out_shape=out_shape...  74.9 us
    pallas_call x2, Pallas kernels, attn_call(): pl.pallas_call(functools.partial(attn_kernel, layer), out_shape=(jax.Shap...  21.5 us

profile of v3, /device:TPU:0, one launch (start us, length us, event | category | flops | bytes accessed | tf_op | source)
XLA Modules:
  0.0 98.9 jit_solution(14885900054172126958)
XLA Ops:
  0.6 0.0 copy-start
  0.6 0.0 copy-start.2
  0.7 0.0 copy-start.3
  0.7 0.0 copy-start.4
  0.7 0.0 copy-start.5
  0.7 0.0 copy-start.6
  0.7 0.0 copy-start.7
  0.7 14.3 %attn0.1 = (f32[4,200,128]{2,1,0:T(8,128)}, bf16[2,64,256,128]{3,2,1,0:T(8,128)(2,1)}, bf16[2,64,256,128]{3,2,1,0:T(8,128)(2,1)}) custom-call(s32[64]{0:T(128)} %pos.3, bf16[64,3072]{1,0:T(8,128)(2,1)} %x.1, bf16[2,2,3072]{2,1,0:T(2,128)(2,1)} %gain.3, bf16[2,2,3072]{2,1,0:T(2,128)(2,1)} %shift.3, bf16[2,2560]{1,0:T(2,128)(2,1)} %rest_0_.3, ...), custom_call_target="tpu_custom_call" | custom-call | tf_op jit(solution)/shard_map/attn0/pallas_call | solution.py:248
  15.0 0.0 copy-done
  15.0 0.0 copy-done.2
  15.0 0.0 copy-done.3
  15.0 0.0 copy-done.4
  15.1 0.0 copy-done.5
  15.1 0.0 copy-done.6
  15.1 0.0 copy-done.7
  15.1 0.0 copy-start.1
  15.1 1.0 %copy-done.1 = f32[4,200,128]{2,1,0:T(8,128)S(1)} copy-done((f32[4,200,128]{2,1,0:T(8,128)S(1)}, f32[4,200,128]{2,1,0:T(8,128)}, u32[]{:S(2)}) %copy-start.1) | copy-done | bytes 409624
  16.1 0.0 copy-start.8
  16.1 39.9 %rest0.1 = (f32[16,3072]{1,0:T(8,128)S(1)}, f32[4,64,640]{2,1,0:T(8,128)S(1)}) custom-call(f32[4,200,128]{2,1,0:T(8,128)S(1)} %copy-done.1, bf16[64,3072]{1,0:T(8,128)(2,1)S(1)} %copy-done, bf16[2,2,3072]{2,1,0:T(2,128)(2,1)S(1)} %copy-done.2, bf16[2,2,3072]{2,1,0:T(2,128)(2,1)S(1)} %copy-done.3, bf16[2,3072]{1,0:T(2,128)(2,1)S(1)} %copy-done.5, ...), custom_call_target="tpu_custom_call" | custom-call | tf_op jit(solution)/shard_map/rest0/pallas_call | solution.py:490
  56.0 0.0 copy-done.8
  56.0 7.2 %attn1.1 = (f32[4,200,128]{2,1,0:T(8,128)S(1)}, bf16[2,64,256,128]{3,2,1,0:T(8,128)(2,1)}, bf16[2,64,256,128]{3,2,1,0:T(8,128)(2,1)}) custom-call(s32[64]{0:T(128)S(1)} %copy-done.8, f32[4,64,640]{2,1,0:T(8,128)S(1)} %get-tuple-element.12.rest_0_, bf16[2,64,256,128]{3,2,1,0:T(8,128)(2,1)} %bitcast.5, ...), custom_call_target="tpu_custom_call", output_to_operand_aliasing={{1}: (4, {}), {2}: (5, {})} | custom-call | tf_op jit(solution)/shard_map/attn1/pallas_call | solution.py:248
  63.1 35.0 %rest1.1 = bf16[64,3072]{1,0:T(8,128)(2,1)S(1)} custom-call(f32[4,200,128]{2,1,0:T(8,128)S(1)} %get-tuple-element.15.msg, f32[16,3072]{1,0:T(8,128)S(1)} %get-tuple-element.16.x, bf16[2,2,3072]{2,1,0:T(2,128)(2,1)S(1)} %copy-done.2, bf16[2,2,3072]{2,1,0:T(2,128)(2,1)S(1)} %copy-done.3, bf16[2,3072]{1,0:T(2,128)(2,1)S(1)} %copy-done.5, ...), custom_call_target="tpu_custom_call" | custom-call | tf_op jit(solution)/shard_map/rest1/pallas_call | solution.py:490
  98.1 0.7 copy.22
Async XLA Ops:
  0.6 14.4 %copy-start = (bf16[64,3072]{1,0:T(8,128)(2,1)S(1)}, bf16[64,3072]{1,0:T(8,128)(2,1)}, u32[]{:S(2)}) copy-start(bf16[64,3072]{1,0:T(8,128)(2,1)} %x.1) | copy-start | bytes 1179652
  0.6 14.4 %copy-start.2 = (bf16[2,2,3072]{2,1,0:T(2,128)(2,1)S(1)}, bf16[2,2,3072]{2,1,0:T(2,128)(2,1)}, u32[]{:S(2)}) copy-start(bf16[2,2,3072]{2,1,0:T(2,128)(2,1)} %gain.3) | copy-start | bytes 73732
  0.7 14.4 %copy-start.3 = (bf16[2,2,3072]{2,1,0:T(2,128)(2,1)S(1)}, bf16[2,2,3072]{2,1,0:T(2,128)(2,1)}, u32[]{:S(2)}) copy-start(bf16[2,2,3072]{2,1,0:T(2,128)(2,1)} %shift.3) | copy-start | bytes 73732
  0.7 14.4 %copy-start.4 = (bf16[2,8192]{1,0:T(2,128)(2,1)S(1)}, bf16[2,8192]{1,0:T(2,128)(2,1)}, u32[]{:S(2)}) copy-start(bf16[2,8192]{1,0:T(2,128)(2,1)} %b_up.3) | copy-start | bytes 98308
  0.7 14.4 %copy-start.5 = (bf16[2,3072]{1,0:T(2,128)(2,1)S(1)}, bf16[2,3072]{1,0:T(2,128)(2,1)}, u32[]{:S(2)}) copy-start(bf16[2,3072]{1,0:T(2,128)(2,1)} %b_dense.3) | copy-start | bytes 36868
  0.7 14.4 %copy-start.6 = (bf16[2,3072]{1,0:T(2,128)(2,1)S(1)}, bf16[2,3072]{1,0:T(2,128)(2,1)}, u32[]{:S(2)}) copy-start(bf16[2,3072]{1,0:T(2,128)(2,1)} %b_down.3) | copy-start | bytes 36868
  0.7 14.4 %copy-start.7 = (bf16[2,2560]{1,0:T(2,128)(2,1)S(1)}, bf16[2,2560]{1,0:T(2,128)(2,1)}, u32[]{:S(2)}) copy-start(bf16[2,2560]{1,0:T(2,128)(2,1)} %rest_0_.3) | copy-start | bytes 30724
  15.1 1.0 %copy-start.1 = (f32[4,200,128]{2,1,0:T(8,128)S(1)}, f32[4,200,128]{2,1,0:T(8,128)}, u32[]{:S(2)}) copy-start(f32[4,200,128]{2,1,0:T(8,128)} %get-tuple-element.11.msg) | copy-start | bytes 1228804
  16.1 39.9 %copy-start.8 = (s32[64]{0:T(128)S(1)}, s32[64]{0:T(128)}, u32[]{:S(2)}) copy-start(s32[64]{0:T(128)} %pos.3) | copy-start | bytes 772

commit v4 on v3

--- a/solution.py
+++ b/solution.py
@@ -29,7 +29,7 @@
 KCS = D // KCH
 G = 8
 NG = NB // G
-GS = 16
+GS = 32
 HALF = NB // 2
 HPC = 6
 MSG = HPC * HALF + 8
@@ -41,9 +41,9 @@
 QCH = 4
 QC = QW // QCH
 DR = HPC * HD
-RCH = 12
+RCH = 6
 RW = D // RCH
-LAG = 5
+LAG = 2
 VMEM_BYTES = 52 * 1024 * 1024
 
 f32 = jnp.float32

time: 99 us -> 96.5 us (0.975)
  Pallas kernels: 96.3 us -> 93.8 us
    pallas_call x2, Pallas kernels: 74.9 us -> 71.3 us  [rest_call(): pl.pallas_call(functools.partial(rest_kernel, layer), out_shape=out_shape...]
where the time goes in v4:
time: 96.5 us; the launch traced here: 96.3 us
  Pallas kernels  93.8 us (97%)
  local copies, waits for them, and re-layouts  1.78 us (2%)
    pallas_call x2, Pallas kernels, rest_call(): pl.pallas_call(functools.partial(rest_kernel, layer), out_shape=out_shape...  71.3 us
    pallas_call x2, Pallas kernels, attn_call(): pl.pallas_call(functools.partial(attn_kernel, layer), out_shape=(jax.Shap...  22.4 us

profile of v4, /device:TPU:0, one launch (start us, length us, event | category | flops | bytes accessed | tf_op | source)
XLA Modules:
  0.0 96.3 jit_solution(7158894280563337970)
XLA Ops:
  0.6 0.0 copy-start
  0.6 0.0 copy-start.2
  0.7 0.0 copy-start.3
  0.7 0.0 copy-start.4
  0.7 0.0 copy-start.5
  0.7 0.0 copy-start.6
  0.7 0.0 copy-start.7
  0.7 14.5 %attn0.1 = (f32[4,200,128]{2,1,0:T(8,128)}, bf16[2,64,256,128]{3,2,1,0:T(8,128)(2,1)}, bf16[2,64,256,128]{3,2,1,0:T(8,128)(2,1)}) custom-call(s32[64]{0:T(128)} %pos.3, bf16[64,3072]{1,0:T(8,128)(2,1)} %x.1, bf16[2,2,3072]{2,1,0:T(2,128)(2,1)} %gain.3, bf16[2,2,3072]{2,1,0:T(2,128)(2,1)} %shift.3, bf16[2,2560]{1,0:T(2,128)(2,1)} %rest_0_.3, ...), custom_call_target="tpu_custom_call" | custom-call | tf_op jit(solution)/shard_map/attn0/pallas_call | solution.py:248
  15.2 0.0 copy-done
  15.2 0.0 copy-done.2
  15.2 0.0 copy-done.3
  15.2 0.0 copy-done.4
  15.3 0.0 copy-done.5
  15.3 0.0 copy-done.6
  15.3 0.0 copy-done.7
  15.3 0.0 copy-start.1
  15.3 1.0 %copy-done.1 = f32[4,200,128]{2,1,0:T(8,128)S(1)} copy-done((f32[4,200,128]{2,1,0:T(8,128)S(1)}, f32[4,200,128]{2,1,0:T(8,128)}, u32[]{:S(2)}) %copy-start.1) | copy-done | bytes 409624
  16.3 0.0 copy-start.8
  16.3 38.0 %rest0.1 = (f32[16,3072]{1,0:T(8,128)S(1)}, f32[4,64,640]{2,1,0:T(8,128)S(1)}) custom-call(f32[4,200,128]{2,1,0:T(8,128)S(1)} %copy-done.1, bf16[64,3072]{1,0:T(8,128)(2,1)S(1)} %copy-done, bf16[2,2,3072]{2,1,0:T(2,128)(2,1)S(1)} %copy-done.2, bf16[2,2,3072]{2,1,0:T(2,128)(2,1)S(1)} %copy-done.3, bf16[2,3072]{1,0:T(2,128)(2,1)S(1)} %copy-done.5, ...), custom_call_target="tpu_custom_call" | custom-call | tf_op jit(solution)/shard_map/rest0/pallas_call | solution.py:490
  54.3 0.0 copy-done.8
  54.3 7.9 %attn1.1 = (f32[4,200,128]{2,1,0:T(8,128)S(1)}, bf16[2,64,256,128]{3,2,1,0:T(8,128)(2,1)}, bf16[2,64,256,128]{3,2,1,0:T(8,128)(2,1)}) custom-call(s32[64]{0:T(128)S(1)} %copy-done.8, f32[4,64,640]{2,1,0:T(8,128)S(1)} %get-tuple-element.12.rest_0_, bf16[2,64,256,128]{3,2,1,0:T(8,128)(2,1)} %bitcast.5, ...), custom_call_target="tpu_custom_call", output_to_operand_aliasing={{1}: (4, {}), {2}: (5, {})} | custom-call | tf_op jit(solution)/shard_map/attn1/pallas_call | solution.py:248
  62.2 33.3 %rest1.1 = bf16[64,3072]{1,0:T(8,128)(2,1)S(1)} custom-call(f32[4,200,128]{2,1,0:T(8,128)S(1)} %get-tuple-element.15.msg, f32[16,3072]{1,0:T(8,128)S(1)} %get-tuple-element.16.x, bf16[2,2,3072]{2,1,0:T(2,128)(2,1)S(1)} %copy-done.2, bf16[2,2,3072]{2,1,0:T(2,128)(2,1)S(1)} %copy-done.3, bf16[2,3072]{1,0:T(2,128)(2,1)S(1)} %copy-done.5, ...), custom_call_target="tpu_custom_call" | custom-call | tf_op jit(solution)/shard_map/rest1/pallas_call | solution.py:490
  95.6 0.7 copy.22
Async XLA Ops:
  0.6 14.6 %copy-start = (bf16[64,3072]{1,0:T(8,128)(2,1)S(1)}, bf16[64,3072]{1,0:T(8,128)(2,1)}, u32[]{:S(2)}) copy-start(bf16[64,3072]{1,0:T(8,128)(2,1)} %x.1) | copy-start | bytes 1179652
  0.6 14.6 %copy-start.2 = (bf16[2,2,3072]{2,1,0:T(2,128)(2,1)S(1)}, bf16[2,2,3072]{2,1,0:T(2,128)(2,1)}, u32[]{:S(2)}) copy-start(bf16[2,2,3072]{2,1,0:T(2,128)(2,1)} %gain.3) | copy-start | bytes 73732
  0.7 14.6 %copy-start.3 = (bf16[2,2,3072]{2,1,0:T(2,128)(2,1)S(1)}, bf16[2,2,3072]{2,1,0:T(2,128)(2,1)}, u32[]{:S(2)}) copy-start(bf16[2,2,3072]{2,1,0:T(2,128)(2,1)} %shift.3) | copy-start | bytes 73732
  0.7 14.6 %copy-start.4 = (bf16[2,8192]{1,0:T(2,128)(2,1)S(1)}, bf16[2,8192]{1,0:T(2,128)(2,1)}, u32[]{:S(2)}) copy-start(bf16[2,8192]{1,0:T(2,128)(2,1)} %b_up.3) | copy-start | bytes 98308
  0.7 14.6 %copy-start.5 = (bf16[2,3072]{1,0:T(2,128)(2,1)S(1)}, bf16[2,3072]{1,0:T(2,128)(2,1)}, u32[]{:S(2)}) copy-start(bf16[2,3072]{1,0:T(2,128)(2,1)} %b_dense.3) | copy-start | bytes 36868
  0.7 14.6 %copy-start.6 = (bf16[2,3072]{1,0:T(2,128)(2,1)S(1)}, bf16[2,3072]{1,0:T(2,128)(2,1)}, u32[]{:S(2)}) copy-start(bf16[2,3072]{1,0:T(2,128)(2,1)} %b_down.3) | copy-start | bytes 36868
  0.7 14.6 %copy-start.7 = (bf16[2,2560]{1,0:T(2,128)(2,1)S(1)}, bf16[2,2560]{1,0:T(2,128)(2,1)}, u32[]{:S(2)}) copy-start(bf16[2,2560]{1,0:T(2,128)(2,1)} %rest_0_.3) | copy-start | bytes 30724
  15.3 1.0 %copy-start.1 = (f32[4,200,128]{2,1,0:T(8,128)S(1)}, f32[4,200,128]{2,1,0:T(8,128)}, u32[]{:S(2)}) copy-start(f32[4,200,128]{2,1,0:T(8,128)} %get-tuple-element.11.msg) | copy-start | bytes 1228804
  16.3 38.0 %copy-start.8 = (s32[64]{0:T(128)S(1)}, s32[64]{0:T(128)}, u32[]{:S(2)}) copy-start(s32[64]{0:T(128)} %pos.3) | copy-start | bytes 772

commit v5 on v4

--- a/solution.py
+++ b/solution.py
@@ -25,11 +25,11 @@
 SLOTS = 64
 QW = KVL * (GRP + 2) * HD
 QROWS = 16
-KCH = 6
+KCH = 12
 KCS = D // KCH
 G = 8
 NG = NB // G
-GS = 32
+GS = 16
 HALF = NB // 2
 HPC = 6
 MSG = HPC * HALF + 8
@@ -96,7 +96,8 @@
             in_copy(vc_hbm, vbuf, vsem, i).start(priority=1)
 
     if layer == 0:
-        w, u, acc, wsem, *places, small_sem = rest
+        w, u, acc, wsem, *places, msg_buf, small_sem = rest
+        msg_hbm, msg = msg, msg_buf
         small = [pltpu.make_async_copy(src, dst, small_sem.at[i]) for i, (src, dst) in enumerate(zip((pos, x, gain, shift, b_qkv), places))]
         for copy in small:
             copy.start()
@@ -155,54 +156,63 @@
     vertical = (sp + head_id + 1) % VERT_STRIDE == 0
     sub_row = lax.broadcasted_iota(jnp.int32, (16, HD), 0) // KVL
 
-    def attn_step(i, carry):
-        copies = [i * (GS // G) + j for j in range(GS // G)]
-        for j in copies:
-            in_copy(kc_hbm, kbuf, ksem, j).wait()
-            in_copy(vc_hbm, vbuf, vsem, j).wait()
-        limits = []
-        for bi in range(GS):
-            b = i * GS + bi
-            p = pos[b]
-            pl_ = p - base
-            pc = jnp.clip(pl_, 0, SLOTS - 1)
-            hit = jnp.logical_and(pl_ >= 0, pl_ < SLOTS)
-            sub = jnp.where(hit, pc % KVL, -1)
-            r0 = pl.multiple_of((pc // KVL) * 16, 16)
-            put = sub_row == sub
-            for buf, new in ((kbuf, kns), (vbuf, vns)):
-                new8 = new[pl.ds(pl.multiple_of(b * 8, 8), 8), :]
-                new16 = jnp.concatenate([new8, new8], axis=0)
-                old = buf[b, pl.ds(r0, 16), :].astype(f32)
-                buf[b, pl.ds(r0, 16), :] = jnp.where(put, new16, old).astype(bf16)
-            if layer == 0:
-                near = p // BLOCK_SIZE - sp < LOCAL_BLOCKS
-                limits.append(jnp.where(vertical, pl_, jnp.where(near, pl_, -1)))
-            else:
-                limits.append(pl_)
-        scores = []
-        for bi in range(GS):
-            b = i * GS + bi
-            q = qs[pl.ds(pl.multiple_of(b * QROWS, QROWS), QROWS), :].astype(bf16)
-            scores.append(lax.dot_general(q, kbuf[b], (((1,), (1,)), ((), ())), preferred_element_type=f32))
-        keeps = [slot_of <= limit for limit in limits]
+    def patch(buf, new, b):
+        at = pos[b] - base
+        atc = jnp.clip(at, 0, SLOTS - 1)
+        hit = jnp.logical_and(at >= 0, at < SLOTS)
+        put = sub_row == jnp.where(hit, atc % KVL, -1)
+        r0 = pl.multiple_of((atc // KVL) * 16, 16)
+        new8 = new[b * 8:b * 8 + 8, :]
+        new16 = jnp.concatenate([new8, new8], axis=0)
+        old = buf[b, pl.ds(r0, 16), :].astype(f32)
+        buf[b, pl.ds(r0, 16), :] = jnp.where(put, new16, old).astype(bf16)
+
+    def score(step):
+        seqs = range(step * GS, (step + 1) * GS)
+        for b in seqs:
+            patch(kbuf, kns, b)
+        return [lax.dot_general(qs[b * QROWS:(b + 1) * QROWS, :].astype(bf16), kbuf[b], (((1,), (1,)), ((), ())),
+                                preferred_element_type=f32) for b in seqs]
+
+    def keep_of(b):
+        at = pos[b] - base
+        if layer == 0:
+            near = pos[b] // BLOCK_SIZE - sp < LOCAL_BLOCKS
+            return slot_of <= jnp.where(vertical, at, jnp.where(near, at, -1))
+        return slot_of <= at
+
+    def mix(step, scores):
+        seqs = range(step * GS, (step + 1) * GS)
+        for b in seqs:
+            patch(vbuf, vns, b)
+        keeps = [keep_of(b) for b in seqs]
         scores = [jnp.where(keep, s * (1.0 / HD), MASKED) for keep, s in zip(keeps, scores)]
         peaks = [jnp.max(s, axis=1, keepdims=True) for s in scores]
         weights = [jnp.where(keep, jnp.exp(s - peak), 0.0) for keep, s, peak in zip(keeps, scores, peaks)]
-        outs = [jnp.dot(wt.astype(bf16), vbuf[i * GS + bi], preferred_element_type=f32) for bi, wt in enumerate(weights)]
+        outs = [jnp.dot(wt.astype(bf16), vbuf[b], preferred_element_type=f32) for b, wt in zip(seqs, weights)]
         sums = [jnp.sum(wt, axis=1, keepdims=True) for wt in weights]
-        for bi in range(GS):
-            rows = pl.ds(pl.multiple_of((i * GS + bi) * QROWS, QROWS), QROWS)
-            ms[rows, :] = jnp.broadcast_to(peaks[bi], (QROWS, HD))
-            ls[rows, :] = jnp.broadcast_to(sums[bi], (QROWS, HD))
-            os[rows, :] = outs[bi]
-
-        for j in copies:
+        for j, b in enumerate(seqs):
+            rows = slice(b * QROWS, (b + 1) * QROWS)
+            ms[rows, :] = jnp.broadcast_to(peaks[j], (QROWS, HD))
+            ls[rows, :] = jnp.broadcast_to(sums[j], (QROWS, HD))
+            os[rows, :] = outs[j]
+
+    per = GS // G
+    steps = NB // GS
+    for j in range(per):
+        in_copy(kc_hbm, kbuf, ksem, j).wait()
+    scores = score(0)
+    for step in range(steps):
+        for j in range(step * per, (step + 1) * per):
+            in_copy(vc_hbm, vbuf, vsem, j).wait()
+            if step + 1 < steps:
+                in_copy(kc_hbm, kbuf, ksem, j + per).wait()
+        later = score(step + 1) if step + 1 < steps else None
+        mix(step, scores)
+        scores = later
+        for j in range(step * per, (step + 1) * per):
             out_copy(kbuf, ko_hbm, 0, j).start()
             out_copy(vbuf, vo_hbm, 1, j).start(priority=1)
-        return carry
-
-    lax.fori_loop(0, NB // GS, attn_step, 0)
 
     lane = lax.broadcasted_iota(jnp.int32, (8, HD), 1)
     for half in range(2):
@@ -216,9 +226,14 @@
                     stat = jnp.where(lane == at, ms[rows, :], stat)
                     stat = jnp.where(lane == at + 1, ls[rows, :], stat)
             msg[half * 2 + c, pl.ds(HPC * HALF, 8), :] = stat
+    if layer == 0:
+        send = pltpu.make_async_copy(msg, msg_hbm, small_sem.at[5])
+        send.start()
     for i in range(NG):
         out_copy(kbuf, ko_hbm, 0, i).wait()
         out_copy(vbuf, vo_hbm, 1, i).wait()
+    if layer == 0:
+        send.wait()
 
 
 def attn_call(layer, pos, operands, k_cache, v_cache, prev):
@@ -235,7 +250,8 @@
             pltpu.SemaphoreType.DMA((KCH,)),
             pltpu.SMEM(pos.shape, jnp.int32),
             *[pltpu.VMEM(arr.shape, bf16) for arr in operands[:4]],
-            pltpu.SemaphoreType.DMA((5,)),
+            pltpu.VMEM((KVL, MSG, HD), f32),
+            pltpu.SemaphoreType.DMA((6,)),
         ]
         limit = 60 * 1024 * 1024
     else:
@@ -249,7 +265,7 @@
         functools.partial(attn_kernel, layer),
         out_shape=(jax.ShapeDtypeStruct((KVL, MSG, HD), f32), cache, cache),
         in_specs=specs,
-        out_specs=(vm, hbm, hbm),
+        out_specs=(hbm if layer == 0 else vm, hbm, hbm),
         scratch_shapes=[
             pltpu.VMEM((NB, SLOTS * KVL, HD), bf16),
             pltpu.VMEM((NB, SLOTS * KVL, HD), bf16),

time: 96.5 us -> 96.4 us (level)
  no operation moved by 1% of the time
where the time goes in v5:
time: 96.4 us; the launch traced here: 96.3 us
  Pallas kernels  93.7 us (97%)
  local copies, waits for them, and re-layouts  1.78 us (2%)
    pallas_call x2, Pallas kernels, rest_call(): pl.pallas_call(functools.partial(rest_kernel, layer), out_shape=out_shape...  71.3 us
    pallas_call x2, Pallas kernels, attn_call(): pl.pallas_call(functools.partial(attn_kernel, layer), out_shape=(jax.Shap...  22.4 us

profile of v5, /device:TPU:0, one launch (start us, length us, event | category | flops | bytes accessed | tf_op | source)
XLA Modules:
  0.0 96.3 jit_solution(12982328330141477135)
XLA Ops:
  0.6 0.0 copy-start
  0.6 0.0 copy-start.2
  0.7 0.0 copy-start.3
  0.7 0.0 copy-start.4
  0.7 0.0 copy-start.5
  0.7 0.0 copy-start.6
  0.7 0.0 copy-start.7
  0.7 15.2 %attn0.1 = (f32[4,200,128]{2,1,0:T(8,128)}, bf16[2,64,256,128]{3,2,1,0:T(8,128)(2,1)}, bf16[2,64,256,128]{3,2,1,0:T(8,128)(2,1)}) custom-call(s32[64]{0:T(128)} %pos.3, bf16[64,3072]{1,0:T(8,128)(2,1)} %x.1, bf16[2,2,3072]{2,1,0:T(2,128)(2,1)} %gain.3, bf16[2,2,3072]{2,1,0:T(2,128)(2,1)} %shift.3, bf16[2,2560]{1,0:T(2,128)(2,1)} %rest_0_.3, ...), custom_call_target="tpu_custom_call" | custom-call | tf_op jit(solution)/shard_map/attn0/pallas_call | solution.py:264
  15.9 0.0 copy-done
  15.9 0.0 copy-done.2
  15.9 0.0 copy-done.3
  15.9 0.0 copy-done.4
  15.9 0.0 copy-done.5
  15.9 0.0 copy-done.6
  16.0 0.0 copy-done.7
  16.0 0.0 copy-start.1
  16.0 1.0 %copy-done.1 = f32[4,200,128]{2,1,0:T(8,128)S(1)} copy-done((f32[4,200,128]{2,1,0:T(8,128)S(1)}, f32[4,200,128]{2,1,0:T(8,128)}, u32[]{:S(2)}) %copy-start.1) | copy-done | bytes 409624
  17.0 0.0 copy-start.8
  17.0 38.0 %rest0.1 = (f32[16,3072]{1,0:T(8,128)S(1)}, f32[4,64,640]{2,1,0:T(8,128)S(1)}) custom-call(f32[4,200,128]{2,1,0:T(8,128)S(1)} %copy-done.1, bf16[64,3072]{1,0:T(8,128)(2,1)S(1)} %copy-done, bf16[2,2,3072]{2,1,0:T(2,128)(2,1)S(1)} %copy-done.2, bf16[2,2,3072]{2,1,0:T(2,128)(2,1)S(1)} %copy-done.3, bf16[2,3072]{1,0:T(2,128)(2,1)S(1)} %copy-done.5, ...), custom_call_target="tpu_custom_call" | custom-call | tf_op jit(solution)/shard_map/rest0/pallas_call | solution.py:506
  55.0 0.0 copy-done.8
  55.0 7.2 %attn1.1 = (f32[4,200,128]{2,1,0:T(8,128)S(1)}, bf16[2,64,256,128]{3,2,1,0:T(8,128)(2,1)}, bf16[2,64,256,128]{3,2,1,0:T(8,128)(2,1)}) custom-call(s32[64]{0:T(128)S(1)} %copy-done.8, f32[4,64,640]{2,1,0:T(8,128)S(1)} %get-tuple-element.12.rest_0_, bf16[2,64,256,128]{3,2,1,0:T(8,128)(2,1)} %bitcast.5, ...), custom_call_target="tpu_custom_call", output_to_operand_aliasing={{1}: (4, {}), {2}: (5, {})} | custom-call | tf_op jit(solution)/shard_map/attn1/pallas_call | solution.py:264
  62.2 33.4 %rest1.1 = bf16[64,3072]{1,0:T(8,128)(2,1)S(1)} custom-call(f32[4,200,128]{2,1,0:T(8,128)S(1)} %get-tuple-element.15.msg, f32[16,3072]{1,0:T(8,128)S(1)} %get-tuple-element.16.x, bf16[2,2,3072]{2,1,0:T(2,128)(2,1)S(1)} %copy-done.2, bf16[2,2,3072]{2,1,0:T(2,128)(2,1)S(1)} %copy-done.3, bf16[2,3072]{1,0:T(2,128)(2,1)S(1)} %copy-done.5, ...), custom_call_target="tpu_custom_call" | custom-call | tf_op jit(solution)/shard_map/rest1/pallas_call | solution.py:506
  95.5 0.7 copy.22
Async XLA Ops:
  0.6 15.3 %copy-start = (bf16[64,3072]{1,0:T(8,128)(2,1)S(1)}, bf16[64,3072]{1,0:T(8,128)(2,1)}, u32[]{:S(2)}) copy-start(bf16[64,3072]{1,0:T(8,128)(2,1)} %x.1) | copy-start | bytes 1179652
  0.6 15.3 %copy-start.2 = (bf16[2,2,3072]{2,1,0:T(2,128)(2,1)S(1)}, bf16[2,2,3072]{2,1,0:T(2,128)(2,1)}, u32[]{:S(2)}) copy-start(bf16[2,2,3072]{2,1,0:T(2,128)(2,1)} %gain.3) | copy-start | bytes 73732
  0.7 15.3 %copy-start.3 = (bf16[2,2,3072]{2,1,0:T(2,128)(2,1)S(1)}, bf16[2,2,3072]{2,1,0:T(2,128)(2,1)}, u32[]{:S(2)}) copy-start(bf16[2,2,3072]{2,1,0:T(2,128)(2,1)} %shift.3) | copy-start | bytes 73732
  0.7 15.3 %copy-start.4 = (bf16[2,8192]{1,0:T(2,128)(2,1)S(1)}, bf16[2,8192]{1,0:T(2,128)(2,1)}, u32[]{:S(2)}) copy-start(bf16[2,8192]{1,0:T(2,128)(2,1)} %b_up.3) | copy-start | bytes 98308
  0.7 15.3 %copy-start.5 = (bf16[2,3072]{1,0:T(2,128)(2,1)S(1)}, bf16[2,3072]{1,0:T(2,128)(2,1)}, u32[]{:S(2)}) copy-start(bf16[2,3072]{1,0:T(2,128)(2,1)} %b_dense.3) | copy-start | bytes 36868
  0.7 15.3 %copy-start.6 = (bf16[2,3072]{1,0:T(2,128)(2,1)S(1)}, bf16[2,3072]{1,0:T(2,128)(2,1)}, u32[]{:S(2)}) copy-start(bf16[2,3072]{1,0:T(2,128)(2,1)} %b_down.3) | copy-start | bytes 36868
  0.7 15.3 %copy-start.7 = (bf16[2,2560]{1,0:T(2,128)(2,1)S(1)}, bf16[2,2560]{1,0:T(2,128)(2,1)}, u32[]{:S(2)}) copy-start(bf16[2,2560]{1,0:T(2,128)(2,1)} %rest_0_.3) | copy-start | bytes 30724
  16.0 1.0 %copy-start.1 = (f32[4,200,128]{2,1,0:T(8,128)S(1)}, f32[4,200,128]{2,1,0:T(8,128)}, u32[]{:S(2)}) copy-start(f32[4,200,128]{2,1,0:T(8,128)} %get-tuple-element.11.msg) | copy-start | bytes 1228804
  17.0 38.0 %copy-start.8 = (s32[64]{0:T(128)S(1)}, s32[64]{0:T(128)}, u32[]{:S(2)}) copy-start(s32[64]{0:T(128)} %pos.3) | copy-start | bytes 772

commit v6 on v5

--- a/solution.py
+++ b/solution.py
@@ -25,7 +25,7 @@
 SLOTS = 64
 QW = KVL * (GRP + 2) * HD
 QROWS = 16
-KCH = 12
+KCH = 6
 KCS = D // KCH
 G = 8
 NG = NB // G
@@ -33,6 +33,7 @@
 HALF = NB // 2
 HPC = 6
 MSG = HPC * HALF + 8
+MSG_ROOM = 160
 ROWS = HALF // 2
 F_LOC = 4096
 M_LOC = F_LOC // 2
@@ -227,7 +228,7 @@
                     stat = jnp.where(lane == at + 1, ls[rows, :], stat)
             msg[half * 2 + c, pl.ds(HPC * HALF, 8), :] = stat
     if layer == 0:
-        send = pltpu.make_async_copy(msg, msg_hbm, small_sem.at[5])
+        send = pltpu.make_async_copy(msg, msg_hbm.at[pl.ds(0, KVL)], small_sem.at[5])
         send.start()
     for i in range(NG):
         out_copy(kbuf, ko_hbm, 0, i).wait()
@@ -263,7 +264,7 @@
     cache = jax.ShapeDtypeStruct(k_cache.shape, bf16)
     return pl.pallas_call(
         functools.partial(attn_kernel, layer),
-        out_shape=(jax.ShapeDtypeStruct((KVL, MSG, HD), f32), cache, cache),
+        out_shape=(jax.ShapeDtypeStruct((MSG_ROOM if layer == 0 else KVL, MSG, HD), f32), cache, cache),
         in_specs=specs,
         out_specs=(hbm if layer == 0 else vm, hbm, hbm),
         scratch_shapes=[
@@ -289,6 +290,7 @@
 def rest_kernel(layer, msg, x, gain, shift, b_dense, b_up, b_down, wd_hbm, wu_hbm, wn_hbm, *rest):
     if layer == 0:
         b_qkv, wq_hbm, x_out, out, *rest = rest
+        msg_hbm, (*rest, msg) = msg, rest
     else:
         out, *rest = rest
     (wd, wu, wn, got, sent, o_buf, part, pair, sums, other, ag, full, xrow, up, mbuf,
@@ -319,11 +321,16 @@
     barrier = pltpu.get_barrier_semaphore()
     for peer in (mate, x_dev, y_dev):
         pl.semaphore_signal(barrier, inc=1, device_id=peer, device_id_type=MESH)
+    if layer == 0:
+        msg_copy = load(msg_hbm.at[pl.ds(0, KVL)], msg, 2 + 2 * NCH)
+        msg_copy.start()
     wd_copy.start()
     for i in range(NCH):
         wu_copy(i).start()
     wn_copy.start()
     pl.semaphore_wait(barrier, 3)
+    if layer == 0:
+        msg_copy.wait()
 
     def remote(src, dst, sems, idx, peer):
         return pltpu.make_async_remote_copy(
@@ -496,7 +503,7 @@
     vm = pl.BlockSpec(memory_space=pltpu.VMEM)
     hbm = pl.BlockSpec(memory_space=pltpu.HBM)
     if layer == 0:
-        in_specs = [vm] * 7 + [hbm] * 3 + [vm, hbm]
+        in_specs = [hbm] + [vm] * 6 + [hbm] * 3 + [vm, hbm]
         out_shape = (jax.ShapeDtypeStruct((ROWS, D), f32), jax.ShapeDtypeStruct((QCH, NB, QC), f32))
         out_specs = (vm, vm)
     else:
@@ -524,12 +531,13 @@
             pltpu.VMEM((ROWS, D), f32),
             pltpu.VMEM((HALF, F_LOC), f32),
             pltpu.VMEM((HALF, M_LOC), bf16),
-            pltpu.SemaphoreType.DMA((2 + 2 * NCH,)),
+            pltpu.SemaphoreType.DMA((3 + 2 * NCH,)),
             pltpu.SemaphoreType.DMA((2, 3)),
             pltpu.SemaphoreType.DMA((2, 2, RCH)),
             pltpu.SemaphoreType.DMA((2, 2, RCH)),
             pltpu.SemaphoreType.DMA((2, NCH)),
             pltpu.SemaphoreType.DMA((2, 3, RCH)),
+            *([pltpu.VMEM((KVL, MSG, HD), f32)] if layer == 0 else []),
         ],
         compiler_params=pltpu.CompilerParams(vmem_limit_bytes=VMEM_BYTES, collective_id=layer, has_side_effects=True),
         name=f'rest{layer}',

time: 96.4 us -> 94.1 us (0.976)
  Pallas kernels: 93.7 us -> 92.4 us
  local copies, waits for them, and re-layouts: 1.78 us -> 0.78 us
    pallas_call x2, Pallas kernels: 22.4 us -> 21 us  [attn_call(): pl.pallas_call(functools.partial(attn_kernel, layer), out_shape=(jax.Shap...]
    unnamed x19 -> x17, local copies, waits for them, and re-layouts: 1.78 us -> 0.78 us
where the time goes in v6:
time: 94.1 us; the launch traced here: 94 us
  Pallas kernels  92.4 us (98%)
    pallas_call x2, Pallas kernels, rest_call(): pl.pallas_call(functools.partial(rest_kernel, layer), out_shape=out_shape...  71.4 us
    pallas_call x2, Pallas kernels, attn_call(): pl.pallas_call(functools.partial(attn_kernel, layer), out_shape=(jax.Shap...  21 us

profile of v6, /device:TPU:0, one launch (start us, length us, event | category | flops | bytes accessed | tf_op | source)
XLA Modules:
  0.0 94.0 jit_solution(8760147583941129753)
XLA Ops:
  0.6 0.0 copy-start
  0.6 0.0 copy-start.1
  0.7 0.0 copy-start.2
  0.7 0.0 copy-start.3
  0.7 0.0 copy-start.4
  0.7 0.0 copy-start.5
  0.7 0.0 copy-start.6
  0.7 13.9 %attn0.1 = (f32[160,200,128]{2,1,0:T(8,128)}, bf16[2,64,256,128]{3,2,1,0:T(8,128)(2,1)}, bf16[2,64,256,128]{3,2,1,0:T(8,128)(2,1)}) custom-call(s32[64]{0:T(128)} %pos.3, bf16[64,3072]{1,0:T(8,128)(2,1)} %x.1, bf16[2,2,3072]{2,1,0:T(2,128)(2,1)} %gain.3, bf16[2,2,3072]{2,1,0:T(2,128)(2,1)} %shift.3, bf16[2,2560]{1,0:T(2,128)(2,1)} %rest_0_.3, ...), custom_call_target="tpu_custom_call" | custom-call | tf_op jit(solution)/shard_map/attn0/pallas_call | solution.py:265
  14.6 0.0 copy-done
  14.6 0.0 copy-done.1
  14.6 0.0 copy-done.2
  14.6 0.0 copy-done.3
  14.6 0.0 copy-done.4
  14.6 0.0 copy-done.5
  14.6 0.0 copy-done.6
  14.6 0.0 copy-start.7
  14.7 38.0 %rest0.1 = (f32[16,3072]{1,0:T(8,128)S(1)}, f32[4,64,640]{2,1,0:T(8,128)S(1)}) custom-call(f32[160,200,128]{2,1,0:T(8,128)} %get-tuple-element.11.msg, bf16[64,3072]{1,0:T(8,128)(2,1)S(1)} %copy-done, bf16[2,2,3072]{2,1,0:T(2,128)(2,1)S(1)} %copy-done.1, bf16[2,2,3072]{2,1,0:T(2,128)(2,1)S(1)} %copy-done.2, bf16[2,3072]{1,0:T(2,128)(2,1)S(1)} %copy-done.4, ...), custom_call_target="tpu_custom_call" | custom-call | tf_op jit(solution)/shard_map/rest0/pallas_call | solution.py:513
  52.7 0.0 copy-done.7
  52.7 7.2 %attn1.1 = (f32[4,200,128]{2,1,0:T(8,128)S(1)}, bf16[2,64,256,128]{3,2,1,0:T(8,128)(2,1)}, bf16[2,64,256,128]{3,2,1,0:T(8,128)(2,1)}) custom-call(s32[64]{0:T(128)S(1)} %copy-done.7, f32[4,64,640]{2,1,0:T(8,128)S(1)} %get-tuple-element.12.rest_0_, bf16[2,64,256,128]{3,2,1,0:T(8,128)(2,1)} %bitcast.5, ...), custom_call_target="tpu_custom_call", output_to_operand_aliasing={{1}: (4, {}), {2}: (5, {})} | custom-call | tf_op jit(solution)/shard_map/attn1/pallas_call | solution.py:265
  59.9 33.4 %rest1.1 = bf16[64,3072]{1,0:T(8,128)(2,1)S(1)} custom-call(f32[4,200,128]{2,1,0:T(8,128)S(1)} %get-tuple-element.15.msg, f32[16,3072]{1,0:T(8,128)S(1)} %get-tuple-element.16.x, bf16[2,2,3072]{2,1,0:T(2,128)(2,1)S(1)} %copy-done.1, bf16[2,2,3072]{2,1,0:T(2,128)(2,1)S(1)} %copy-done.2, bf16[2,3072]{1,0:T(2,128)(2,1)S(1)} %copy-done.4, ...), custom_call_target="tpu_custom_call" | custom-call | tf_op jit(solution)/shard_map/rest1/pallas_call | solution.py:513
  93.3 0.7 copy.22
Async XLA Ops:
  0.6 13.9 %copy-start = (bf16[64,3072]{1,0:T(8,128)(2,1)S(1)}, bf16[64,3072]{1,0:T(8,128)(2,1)}, u32[]{:S(2)}) copy-start(bf16[64,3072]{1,0:T(8,128)(2,1)} %x.1) | copy-start | bytes 1179652
  0.6 13.9 %copy-start.1 = (bf16[2,2,3072]{2,1,0:T(2,128)(2,1)S(1)}, bf16[2,2,3072]{2,1,0:T(2,128)(2,1)}, u32[]{:S(2)}) copy-start(bf16[2,2,3072]{2,1,0:T(2,128)(2,1)} %gain.3) | copy-start | bytes 73732
  0.7 13.9 %copy-start.2 = (bf16[2,2,3072]{2,1,0:T(2,128)(2,1)S(1)}, bf16[2,2,3072]{2,1,0:T(2,128)(2,1)}, u32[]{:S(2)}) copy-start(bf16[2,2,3072]{2,1,0:T(2,128)(2,1)} %shift.3) | copy-start | bytes 73732
  0.7 13.9 %copy-start.3 = (bf16[2,8192]{1,0:T(2,128)(2,1)S(1)}, bf16[2,8192]{1,0:T(2,128)(2,1)}, u32[]{:S(2)}) copy-start(bf16[2,8192]{1,0:T(2,128)(2,1)} %b_up.3) | copy-start | bytes 98308
  0.7 13.9 %copy-start.4 = (bf16[2,3072]{1,0:T(2,128)(2,1)S(1)}, bf16[2,3072]{1,0:T(2,128)(2,1)}, u32[]{:S(2)}) copy-start(bf16[2,3072]{1,0:T(2,128)(2,1)} %b_dense.3) | copy-start | bytes 36868
  0.7 13.9 %copy-start.5 = (bf16[2,3072]{1,0:T(2,128)(2,1)S(1)}, bf16[2,3072]{1,0:T(2,128)(2,1)}, u32[]{:S(2)}) copy-start(bf16[2,3072]{1,0:T(2,128)(2,1)} %b_down.3) | copy-start | bytes 36868
  0.7 13.9 %copy-start.6 = (bf16[2,2560]{1,0:T(2,128)(2,1)S(1)}, bf16[2,2560]{1,0:T(2,128)(2,1)}, u32[]{:S(2)}) copy-start(bf16[2,2560]{1,0:T(2,128)(2,1)} %rest_0_.3) | copy-start | bytes 30724
  14.6 38.1 %copy-start.7 = (s32[64]{0:T(128)S(1)}, s32[64]{0:T(128)}, u32[]{:S(2)}) copy-start(s32[64]{0:T(128)} %pos.3) | copy-start | bytes 772

commit v7 on v6

--- a/solution.py
+++ b/solution.py
@@ -37,9 +37,9 @@
 ROWS = HALF // 2
 F_LOC = 4096
 M_LOC = F_LOC // 2
-NCH = 6
+NCH = 3
 CW = D // NCH
-QCH = 4
+QCH = 5
 QC = QW // QCH
 DR = HPC * HD
 RCH = 6
@@ -138,7 +138,8 @@
                 col = (c * (GRP + 2) + j) * HD
                 tile = acc[:, col:col + HD]
             else:
-                tile = acc[c, :, j * HD:(j + 1) * HD]
+                head = c * (GRP + 2) + j
+                tile = acc[head // (QC // HD), :, head % (QC // HD) * HD:(head % (QC // HD) + 1) * HD]
             if j <= GRP:
                 tile = tile * cos_t + pltpu.roll(tile, HD // 2, 1) * sin_t
             for i in range(NB // 8):
@@ -212,7 +213,10 @@
         mix(step, scores)
         scores = later
         for j in range(step * per, (step + 1) * per):
-            out_copy(kbuf, ko_hbm, 0, j).start()
+            if step == 0:
+                out_copy(kbuf, ko_hbm, 0, j).start()
+            if step + 1 < steps:
+                out_copy(kbuf, ko_hbm, 0, j + per).start()
             out_copy(vbuf, vo_hbm, 1, j).start(priority=1)
 
     lane = lax.broadcasted_iota(jnp.int32, (8, HD), 1)

time: 94.1 us -> 93.5 us (level)
  no operation moved by 1% of the time
where the time goes in v7:
time: 93.5 us; the launch traced here: 93.4 us
  Pallas kernels  91.8 us (98%)
    pallas_call x2, Pallas kernels, rest_call(): pl.pallas_call(functools.partial(rest_kernel, layer), out_shape=out_shape...  71.1 us
    pallas_call x2, Pallas kernels, attn_call(): pl.pallas_call(functools.partial(attn_kernel, layer), out_shape=(jax.Shap...  20.7 us

profile of v7, /device:TPU:0, one launch (start us, length us, event | category | flops | bytes accessed | tf_op | source)
XLA Modules:
  0.0 93.4 jit_solution(17841050756146647861)
XLA Ops:
  0.6 0.0 copy-start
  0.6 0.0 copy-start.1
  0.7 0.0 copy-start.2
  0.7 0.0 copy-start.3
  0.7 0.0 copy-start.4
  0.7 0.0 copy-start.5
  0.7 0.0 copy-start.6
  0.7 13.7 %attn0.1 = (f32[160,200,128]{2,1,0:T(8,128)}, bf16[2,64,256,128]{3,2,1,0:T(8,128)(2,1)}, bf16[2,64,256,128]{3,2,1,0:T(8,128)(2,1)}) custom-call(s32[64]{0:T(128)} %pos.3, bf16[64,3072]{1,0:T(8,128)(2,1)} %x.1, bf16[2,2,3072]{2,1,0:T(2,128)(2,1)} %gain.3, bf16[2,2,3072]{2,1,0:T(2,128)(2,1)} %shift.3, bf16[2,2560]{1,0:T(2,128)(2,1)} %rest_0_.3, ...), custom_call_target="tpu_custom_call" | custom-call | tf_op jit(solution)/shard_map/attn0/pallas_call | solution.py:269
  14.4 0.0 copy-done
  14.4 0.0 copy-done.1
  14.4 0.0 copy-done.2
  14.4 0.0 copy-done.3
  14.4 0.0 copy-done.4
  14.4 0.0 copy-done.5
  14.4 0.0 copy-done.6
  14.4 0.0 copy-start.7
  14.4 37.9 %rest0.1 = (f32[16,3072]{1,0:T(8,128)S(1)}, f32[5,64,512]{2,1,0:T(8,128)S(1)}) custom-call(f32[160,200,128]{2,1,0:T(8,128)} %get-tuple-element.11.msg, bf16[64,3072]{1,0:T(8,128)(2,1)S(1)} %copy-done, bf16[2,2,3072]{2,1,0:T(2,128)(2,1)S(1)} %copy-done.1, bf16[2,2,3072]{2,1,0:T(2,128)(2,1)S(1)} %copy-done.2, bf16[2,3072]{1,0:T(2,128)(2,1)S(1)} %copy-done.4, ...), custom_call_target="tpu_custom_call" | custom-call | tf_op jit(solution)/shard_map/rest0/pallas_call | solution.py:517
  52.3 0.0 copy-done.7
  52.3 7.0 %attn1.1 = (f32[4,200,128]{2,1,0:T(8,128)S(1)}, bf16[2,64,256,128]{3,2,1,0:T(8,128)(2,1)}, bf16[2,64,256,128]{3,2,1,0:T(8,128)(2,1)}) custom-call(s32[64]{0:T(128)S(1)} %copy-done.7, f32[5,64,512]{2,1,0:T(8,128)S(1)} %get-tuple-element.12.rest_0_, bf16[2,64,256,128]{3,2,1,0:T(8,128)(2,1)} %bitcast.5, ...), custom_call_target="tpu_custom_call", output_to_operand_aliasing={{1}: (4, {}), {2}: (5, {})} | custom-call | tf_op jit(solution)/shard_map/attn1/pallas_call | solution.py:269
  59.3 33.3 %rest1.1 = bf16[64,3072]{1,0:T(8,128)(2,1)S(1)} custom-call(f32[4,200,128]{2,1,0:T(8,128)S(1)} %get-tuple-element.15.msg, f32[16,3072]{1,0:T(8,128)S(1)} %get-tuple-element.16.x, bf16[2,2,3072]{2,1,0:T(2,128)(2,1)S(1)} %copy-done.1, bf16[2,2,3072]{2,1,0:T(2,128)(2,1)S(1)} %copy-done.2, bf16[2,3072]{1,0:T(2,128)(2,1)S(1)} %copy-done.4, ...), custom_call_target="tpu_custom_call" | custom-call | tf_op jit(solution)/shard_map/rest1/pallas_call | solution.py:517
  92.6 0.7 copy.22
Async XLA Ops:
  0.6 13.7 %copy-start = (bf16[64,3072]{1,0:T(8,128)(2,1)S(1)}, bf16[64,3072]{1,0:T(8,128)(2,1)}, u32[]{:S(2)}) copy-start(bf16[64,3072]{1,0:T(8,128)(2,1)} %x.1) | copy-start | bytes 1179652
  0.6 13.7 %copy-start.1 = (bf16[2,2,3072]{2,1,0:T(2,128)(2,1)S(1)}, bf16[2,2,3072]{2,1,0:T(2,128)(2,1)}, u32[]{:S(2)}) copy-start(bf16[2,2,3072]{2,1,0:T(2,128)(2,1)} %gain.3) | copy-start | bytes 73732
  0.7 13.7 %copy-start.2 = (bf16[2,2,3072]{2,1,0:T(2,128)(2,1)S(1)}, bf16[2,2,3072]{2,1,0:T(2,128)(2,1)}, u32[]{:S(2)}) copy-start(bf16[2,2,3072]{2,1,0:T(2,128)(2,1)} %shift.3) | copy-start | bytes 73732
  0.7 13.7 %copy-start.3 = (bf16[2,8192]{1,0:T(2,128)(2,1)S(1)}, bf16[2,8192]{1,0:T(2,128)(2,1)}, u32[]{:S(2)}) copy-start(bf16[2,8192]{1,0:T(2,128)(2,1)} %b_up.3) | copy-start | bytes 98308
  0.7 13.7 %copy-start.4 = (bf16[2,3072]{1,0:T(2,128)(2,1)S(1)}, bf16[2,3072]{1,0:T(2,128)(2,1)}, u32[]{:S(2)}) copy-start(bf16[2,3072]{1,0:T(2,128)(2,1)} %b_dense.3) | copy-start | bytes 36868
  0.7 13.7 %copy-start.5 = (bf16[2,3072]{1,0:T(2,128)(2,1)S(1)}, bf16[2,3072]{1,0:T(2,128)(2,1)}, u32[]{:S(2)}) copy-start(bf16[2,3072]{1,0:T(2,128)(2,1)} %b_down.3) | copy-start | bytes 36868
  0.7 13.7 %copy-start.6 = (bf16[2,2560]{1,0:T(2,128)(2,1)S(1)}, bf16[2,2560]{1,0:T(2,128)(2,1)}, u32[]{:S(2)}) copy-start(bf16[2,2560]{1,0:T(2,128)(2,1)} %rest_0_.3) | copy-start | bytes 30724
  14.4 37.9 %copy-start.7 = (s32[64]{0:T(128)S(1)}, s32[64]{0:T(128)}, u32[]{:S(2)}) copy-start(s32[64]{0:T(128)} %pos.3) | copy-start | bytes 772

commit v8 on v7

--- a/solution.py
+++ b/solution.py
@@ -32,7 +32,8 @@
 GS = 16
 HALF = NB // 2
 HPC = 6
-MSG = HPC * HALF + 8
+PART = HPC // 2 * HALF + 8
+MSG = 2 * PART
 MSG_ROOM = 160
 ROWS = HALF // 2
 F_LOC = 4096
@@ -222,15 +223,17 @@
     lane = lax.broadcasted_iota(jnp.int32, (8, HD), 1)
     for half in range(2):
         for c in range(2):
-            stat = jnp.zeros((8, HD), f32)
-            for g in range(HPC):
-                for i in range(HALF // 8):
-                    rows = pl.ds((half * HALF + i * 8) * QROWS + c * HPC + g, 8, stride=QROWS)
-                    at = 2 * (g * (HALF // 8) + i)
-                    msg[half * 2 + c, pl.ds(g * HALF + i * 8, 8), :] = os[rows, :]
-                    stat = jnp.where(lane == at, ms[rows, :], stat)
-                    stat = jnp.where(lane == at + 1, ls[rows, :], stat)
-            msg[half * 2 + c, pl.ds(HPC * HALF, 8), :] = stat
+            for part in range(2):
+                stat = jnp.zeros((8, HD), f32)
+                for g in range(HPC // 2):
+                    for i in range(HALF // 8):
+                        head = c * HPC + part * (HPC // 2) + g
+                        rows = pl.ds((half * HALF + i * 8) * QROWS + head, 8, stride=QROWS)
+                        at = 2 * (g * (HALF // 8) + i)
+                        msg[half * 2 + c, pl.ds(part * PART + g * HALF + i * 8, 8), :] = os[rows, :]
+                        stat = jnp.where(lane == at, ms[rows, :], stat)
+                        stat = jnp.where(lane == at + 1, ls[rows, :], stat)
+                msg[half * 2 + c, pl.ds(part * PART + PART - 8, 8), :] = stat
     if layer == 0:
         send = pltpu.make_async_copy(msg, msg_hbm.at[pl.ds(0, KVL)], small_sem.at[5])
         send.start()
@@ -343,9 +346,11 @@
 
     near = cx * 2 + core
     far = ox * 2 + core
-    swap = [remote(msg.at[ox * 2 + 1 - core], got.at[0], a_sem, (0,), mate),
-            remote(msg.at[cx * 2 + 1 - core], got.at[1], a_sem, (1,), mate)]
-    for copy in swap:
+    parts = [pl.ds(k * PART, PART) for k in range(2)]
+    swap = [[remote(msg.at[home, parts[k], :], got.at[j, parts[k], :], a_sem, (2 * j + k,), mate) for k in range(2)]
+            for j, home in enumerate((ox * 2 + 1 - core, cx * 2 + 1 - core))]
+    cross = [remote(sent.at[0, parts[k], :], got.at[2, parts[k], :], a_sem, (4 + k,), x_dev) for k in range(2)]
+    for copy in swap[0] + swap[1]:
         copy.start()
 
     gain1 = gain[layer, 1:2, :].astype(f32)
@@ -359,43 +364,46 @@
     xrow[...] = x[all_rows(cx, core), :].astype(f32) if layer == 0 else x[...]
     lane = lax.broadcasted_iota(jnp.int32, (8, HD), 1)
 
-    def merge(one, two, put, stat_out=None):
-        stats = [ref[pl.ds(HPC * HALF, 8), :] for ref in (one, two)]
+    def merge(one, two, k, put, stat_out=None):
+        stats = [ref[pl.ds(k * PART + PART - 8, 8), :] for ref in (one, two)]
         new_stat = jnp.zeros((8, HD), f32)
-        for g in range(HPC):
+        for g in range(HPC // 2):
             for i in range(HALF // 8):
                 at = 2 * (g * (HALF // 8) + i)
                 peaks = [jnp.broadcast_to(st[:, at:at + 1], (8, HD)) for st in stats]
                 tots = [jnp.broadcast_to(st[:, at + 1:at + 2], (8, HD)) for st in stats]
                 top = jnp.maximum(peaks[0], peaks[1])
                 scale = [jnp.exp(p - top) for p in peaks]
-                rows = pl.ds(g * HALF + i * 8, 8)
+                rows = pl.ds(k * PART + g * HALF + i * 8, 8)
                 num = one[rows, :] * scale[0] + two[rows, :] * scale[1]
                 den = tots[0] * scale[0] + tots[1] * scale[1]
-                put(g, i, num, den)
+                put(k, g, i, num, den)
                 if stat_out is not None:
                     new_stat = jnp.where(lane == at, top, new_stat)
                     new_stat = jnp.where(lane == at + 1, den, new_stat)
         if stat_out is not None:
-            stat_out[pl.ds(HPC * HALF, 8), :] = new_stat
+            stat_out[pl.ds(k * PART + PART - 8, 8), :] = new_stat
 
     def put_part(ref):
-        def put(g, i, num, den):
-            ref[pl.ds(g * HALF + i * 8, 8), :] = num
+        def put(k, g, i, num, den):
+            ref[pl.ds(k * PART + g * HALF + i * 8, 8), :] = num
         return put
 
-    def put_out(g, i, num, den):
-        o_buf[pl.ds(i * 8, 8), g * HD:(g + 1) * HD] = num / den
-
-    swap[0].wait_recv()
-    merge(msg.at[far], got.at[0], put_part(sent.at[0]), sent.at[0])
-    cross = remote(sent.at[0], got.at[2], a_sem, (2,), x_dev)
-    cross.start()
-    swap[1].wait_recv()
-    merge(msg.at[near], got.at[1], put_part(sent.at[1]), sent.at[1])
-    cross.wait_recv()
-    merge(sent.at[1], got.at[2], put_out)
-    sends = swap + [cross]
+    def put_out(k, g, i, num, den):
+        head = k * (HPC // 2) + g
+        o_buf[pl.ds(i * 8, 8), head * HD:(head + 1) * HD] = num / den
+
+    for k in range(2):
+        swap[0][k].wait_recv()
+        merge(msg.at[far], got.at[0], k, put_part(sent.at[0]), sent.at[0])
+        cross[k].start()
+    for k in range(2):
+        swap[1][k].wait_recv()
+        merge(msg.at[near], got.at[1], k, put_part(sent.at[1]), sent.at[1])
+    for k in range(2):
+        cross[k].wait_recv()
+        merge(sent.at[1], got.at[2], k, put_out)
+    sends = swap[0] + swap[1] + cross
 
     def reduce(ph, product, finish):
         first = [remote(part.at[ph, n, theirs, :], pair.at[ph, n], d_sem, (ph, n), mate) for n in range(RCH)]
@@ -536,7 +544,7 @@
             pltpu.VMEM((HALF, F_LOC), f32),
             pltpu.VMEM((HALF, M_LOC), bf16),
             pltpu.SemaphoreType.DMA((3 + 2 * NCH,)),
-            pltpu.SemaphoreType.DMA((2, 3)),
+            pltpu.SemaphoreType.DMA((2, 6)),
             pltpu.SemaphoreType.DMA((2, 2, RCH)),
             pltpu.SemaphoreType.DMA((2, 2, RCH)),
             pltpu.SemaphoreType.DMA((2, NCH)),

time: 93.5 us -> 93.3 us (level)
  no operation moved by 1% of the time
where the time goes in v8:
time: 93.3 us; the launch traced here: 93.2 us
  Pallas kernels  91.6 us (98%)
    pallas_call x2, Pallas kernels, rest_call(): pl.pallas_call(functools.partial(rest_kernel, layer), out_shape=out_shape...  71 us
    pallas_call x2, Pallas kernels, attn_call(): pl.pallas_call(functools.partial(attn_kernel, layer), out_shape=(jax.Shap...  20.7 us

profile of v8, /device:TPU:0, one launch (start us, length us, event | category | flops | bytes accessed | tf_op | source)
XLA Modules:
  0.0 93.2 jit_solution(10098750412202713660)
XLA Ops:
  0.6 0.0 copy-start
  0.6 0.0 copy-start.1
  0.7 0.0 copy-start.2
  0.7 0.0 copy-start.3
  0.7 0.0 copy-start.4
  0.7 0.0 copy-start.5
  0.7 0.0 copy-start.6
  0.7 13.7 %attn0.1 = (f32[160,208,128]{2,1,0:T(8,128)}, bf16[2,64,256,128]{3,2,1,0:T(8,128)(2,1)}, bf16[2,64,256,128]{3,2,1,0:T(8,128)(2,1)}) custom-call(s32[64]{0:T(128)} %pos.3, bf16[64,3072]{1,0:T(8,128)(2,1)} %x.1, bf16[2,2,3072]{2,1,0:T(2,128)(2,1)} %gain.3, bf16[2,2,3072]{2,1,0:T(2,128)(2,1)} %shift.3, bf16[2,2560]{1,0:T(2,128)(2,1)} %rest_0_.3, ...), custom_call_target="tpu_custom_call" | custom-call | tf_op jit(solution)/shard_map/attn0/pallas_call | solution.py:272
  14.4 0.0 copy-done
  14.4 0.0 copy-done.1
  14.4 0.0 copy-done.2
  14.4 0.0 copy-done.3
  14.4 0.0 copy-done.4
  14.4 0.0 copy-done.5
  14.4 0.0 copy-done.6
  14.4 0.0 copy-start.7
  14.5 37.8 %rest0.1 = (f32[16,3072]{1,0:T(8,128)S(1)}, f32[5,64,512]{2,1,0:T(8,128)S(1)}) custom-call(f32[160,208,128]{2,1,0:T(8,128)} %get-tuple-element.11.msg, bf16[64,3072]{1,0:T(8,128)(2,1)S(1)} %copy-done, bf16[2,2,3072]{2,1,0:T(2,128)(2,1)S(1)} %copy-done.1, bf16[2,2,3072]{2,1,0:T(2,128)(2,1)S(1)} %copy-done.2, bf16[2,3072]{1,0:T(2,128)(2,1)S(1)} %copy-done.4, ...), custom_call_target="tpu_custom_call" | custom-call | tf_op jit(solution)/shard_map/rest0/pallas_call | solution.py:525
  52.2 0.0 copy-done.7
  52.2 7.0 %attn1.1 = (f32[4,208,128]{2,1,0:T(8,128)S(1)}, bf16[2,64,256,128]{3,2,1,0:T(8,128)(2,1)}, bf16[2,64,256,128]{3,2,1,0:T(8,128)(2,1)}) custom-call(s32[64]{0:T(128)S(1)} %copy-done.7, f32[5,64,512]{2,1,0:T(8,128)S(1)} %get-tuple-element.12.rest_0_, bf16[2,64,256,128]{3,2,1,0:T(8,128)(2,1)} %bitcast.5, ...), custom_call_target="tpu_custom_call", output_to_operand_aliasing={{1}: (4, {}), {2}: (5, {})} | custom-call | tf_op jit(solution)/shard_map/attn1/pallas_call | solution.py:272
  59.2 33.2 %rest1.1 = bf16[64,3072]{1,0:T(8,128)(2,1)S(1)} custom-call(f32[4,208,128]{2,1,0:T(8,128)S(1)} %get-tuple-element.15.msg, f32[16,3072]{1,0:T(8,128)S(1)} %get-tuple-element.16.x, bf16[2,2,3072]{2,1,0:T(2,128)(2,1)S(1)} %copy-done.1, bf16[2,2,3072]{2,1,0:T(2,128)(2,1)S(1)} %copy-done.2, bf16[2,3072]{1,0:T(2,128)(2,1)S(1)} %copy-done.4, ...), custom_call_target="tpu_custom_call" | custom-call | tf_op jit(solution)/shard_map/rest1/pallas_call | solution.py:525
  92.4 0.7 copy.22
Async XLA Ops:
  0.6 13.7 %copy-start = (bf16[64,3072]{1,0:T(8,128)(2,1)S(1)}, bf16[64,3072]{1,0:T(8,128)(2,1)}, u32[]{:S(2)}) copy-start(bf16[64,3072]{1,0:T(8,128)(2,1)} %x.1) | copy-start | bytes 1179652
  0.6 13.7 %copy-start.1 = (bf16[2,2,3072]{2,1,0:T(2,128)(2,1)S(1)}, bf16[2,2,3072]{2,1,0:T(2,128)(2,1)}, u32[]{:S(2)}) copy-start(bf16[2,2,3072]{2,1,0:T(2,128)(2,1)} %gain.3) | copy-start | bytes 73732
  0.7 13.7 %copy-start.2 = (bf16[2,2,3072]{2,1,0:T(2,128)(2,1)S(1)}, bf16[2,2,3072]{2,1,0:T(2,128)(2,1)}, u32[]{:S(2)}) copy-start(bf16[2,2,3072]{2,1,0:T(2,128)(2,1)} %shift.3) | copy-start | bytes 73732
  0.7 13.7 %copy-start.3 = (bf16[2,8192]{1,0:T(2,128)(2,1)S(1)}, bf16[2,8192]{1,0:T(2,128)(2,1)}, u32[]{:S(2)}) copy-start(bf16[2,8192]{1,0:T(2,128)(2,1)} %b_up.3) | copy-start | bytes 98308
  0.7 13.7 %copy-start.4 = (bf16[2,3072]{1,0:T(2,128)(2,1)S(1)}, bf16[2,3072]{1,0:T(2,128)(2,1)}, u32[]{:S(2)}) copy-start(bf16[2,3072]{1,0:T(2,128)(2,1)} %b_dense.3) | copy-start | bytes 36868
  0.7 13.7 %copy-start.5 = (bf16[2,3072]{1,0:T(2,128)(2,1)S(1)}, bf16[2,3072]{1,0:T(2,128)(2,1)}, u32[]{:S(2)}) copy-start(bf16[2,3072]{1,0:T(2,128)(2,1)} %b_down.3) | copy-start | bytes 36868
  0.7 13.7 %copy-start.6 = (bf16[2,2560]{1,0:T(2,128)(2,1)S(1)}, bf16[2,2560]{1,0:T(2,128)(2,1)}, u32[]{:S(2)}) copy-start(bf16[2,2560]{1,0:T(2,128)(2,1)} %rest_0_.3) | copy-start | bytes 30724
  14.4 37.8 %copy-start.7 = (s32[64]{0:T(128)S(1)}, s32[64]{0:T(128)}, u32[]{:S(2)}) copy-start(s32[64]{0:T(128)} %pos.3) | copy-start | bytes 772

commit v9 on v8

--- a/solution.py
+++ b/solution.py
@@ -38,7 +38,7 @@
 ROWS = HALF // 2
 F_LOC = 4096
 M_LOC = F_LOC // 2
-NCH = 3
+NCH = 2
 CW = D // NCH
 QCH = 5
 QC = QW // QCH

time: 93.3 us -> 93.3 us (level)
  no operation moved by 1% of the time
where the time goes in v9:
time: 93.3 us; the launch traced here: 93.2 us
  Pallas kernels  91.6 us (98%)
    pallas_call x2, Pallas kernels, rest_call(): pl.pallas_call(functools.partial(rest_kernel, layer), out_shape=out_shape...  71 us
    pallas_call x2, Pallas kernels, attn_call(): pl.pallas_call(functools.partial(attn_kernel, layer), out_shape=(jax.Shap...  20.7 us

profile of v9, /device:TPU:0, one launch (start us, length us, event | category | flops | bytes accessed | tf_op | source)
XLA Modules:
  0.0 93.2 jit_solution(14320715570084805680)
XLA Ops:
  0.6 0.0 copy-start
  0.6 0.0 copy-start.1
  0.7 0.0 copy-start.2
  0.7 0.0 copy-start.3
  0.7 0.0 copy-start.4
  0.7 0.0 copy-start.5
  0.7 0.0 copy-start.6
  0.7 13.7 %attn0.1 = (f32[160,208,128]{2,1,0:T(8,128)}, bf16[2,64,256,128]{3,2,1,0:T(8,128)(2,1)}, bf16[2,64,256,128]{3,2,1,0:T(8,128)(2,1)}) custom-call(s32[64]{0:T(128)} %pos.3, bf16[64,3072]{1,0:T(8,128)(2,1)} %x.1, bf16[2,2,3072]{2,1,0:T(2,128)(2,1)} %gain.3, bf16[2,2,3072]{2,1,0:T(2,128)(2,1)} %shift.3, bf16[2,2560]{1,0:T(2,128)(2,1)} %rest_0_.3, ...), custom_call_target="tpu_custom_call" | custom-call | tf_op jit(solution)/shard_map/attn0/pallas_call | solution.py:272
  14.4 0.0 copy-done
  14.4 0.0 copy-done.1
  14.4 0.0 copy-done.2
  14.4 0.0 copy-done.3
  14.4 0.0 copy-done.4
  14.4 0.0 copy-done.5
  14.4 0.0 copy-done.6
  14.4 0.0 copy-start.7
  14.5 37.8 %rest0.1 = (f32[16,3072]{1,0:T(8,128)S(1)}, f32[5,64,512]{2,1,0:T(8,128)S(1)}) custom-call(f32[160,208,128]{2,1,0:T(8,128)} %get-tuple-element.11.msg, bf16[64,3072]{1,0:T(8,128)(2,1)S(1)} %copy-done, bf16[2,2,3072]{2,1,0:T(2,128)(2,1)S(1)} %copy-done.1, bf16[2,2,3072]{2,1,0:T(2,128)(2,1)S(1)} %copy-done.2, bf16[2,3072]{1,0:T(2,128)(2,1)S(1)} %copy-done.4, ...), custom_call_target="tpu_custom_call" | custom-call | tf_op jit(solution)/shard_map/rest0/pallas_call | solution.py:525
  52.2 0.0 copy-done.7
  52.2 7.0 %attn1.1 = (f32[4,208,128]{2,1,0:T(8,128)S(1)}, bf16[2,64,256,128]{3,2,1,0:T(8,128)(2,1)}, bf16[2,64,256,128]{3,2,1,0:T(8,128)(2,1)}) custom-call(s32[64]{0:T(128)S(1)} %copy-done.7, f32[5,64,512]{2,1,0:T(8,128)S(1)} %get-tuple-element.12.rest_0_, bf16[2,64,256,128]{3,2,1,0:T(8,128)(2,1)} %bitcast.5, ...), custom_call_target="tpu_custom_call", output_to_operand_aliasing={{1}: (4, {}), {2}: (5, {})} | custom-call | tf_op jit(solution)/shard_map/attn1/pallas_call | solution.py:272
  59.3 33.2 %rest1.1 = bf16[64,3072]{1,0:T(8,128)(2,1)S(1)} custom-call(f32[4,208,128]{2,1,0:T(8,128)S(1)} %get-tuple-element.15.msg, f32[16,3072]{1,0:T(8,128)S(1)} %get-tuple-element.16.x, bf16[2,2,3072]{2,1,0:T(2,128)(2,1)S(1)} %copy-done.1, bf16[2,2,3072]{2,1,0:T(2,128)(2,1)S(1)} %copy-done.2, bf16[2,3072]{1,0:T(2,128)(2,1)S(1)} %copy-done.4, ...), custom_call_target="tpu_custom_call" | custom-call | tf_op jit(solution)/shard_map/rest1/pallas_call | solution.py:525
  92.5 0.7 copy.22
Async XLA Ops:
  0.6 13.7 %copy-start = (bf16[64,3072]{1,0:T(8,128)(2,1)S(1)}, bf16[64,3072]{1,0:T(8,128)(2,1)}, u32[]{:S(2)}) copy-start(bf16[64,3072]{1,0:T(8,128)(2,1)} %x.1) | copy-start | bytes 1179652
  0.6 13.7 %copy-start.1 = (bf16[2,2,3072]{2,1,0:T(2,128)(2,1)S(1)}, bf16[2,2,3072]{2,1,0:T(2,128)(2,1)}, u32[]{:S(2)}) copy-start(bf16[2,2,3072]{2,1,0:T(2,128)(2,1)} %gain.3) | copy-start | bytes 73732
  0.7 13.7 %copy-start.2 = (bf16[2,2,3072]{2,1,0:T(2,128)(2,1)S(1)}, bf16[2,2,3072]{2,1,0:T(2,128)(2,1)}, u32[]{:S(2)}) copy-start(bf16[2,2,3072]{2,1,0:T(2,128)(2,1)} %shift.3) | copy-start | bytes 73732
  0.7 13.7 %copy-start.3 = (bf16[2,8192]{1,0:T(2,128)(2,1)S(1)}, bf16[2,8192]{1,0:T(2,128)(2,1)}, u32[]{:S(2)}) copy-start(bf16[2,8192]{1,0:T(2,128)(2,1)} %b_up.3) | copy-start | bytes 98308
  0.7 13.7 %copy-start.4 = (bf16[2,3072]{1,0:T(2,128)(2,1)S(1)}, bf16[2,3072]{1,0:T(2,128)(2,1)}, u32[]{:S(2)}) copy-start(bf16[2,3072]{1,0:T(2,128)(2,1)} %b_dense.3) | copy-start | bytes 36868
  0.7 13.7 %copy-start.5 = (bf16[2,3072]{1,0:T(2,128)(2,1)S(1)}, bf16[2,3072]{1,0:T(2,128)(2,1)}, u32[]{:S(2)}) copy-start(bf16[2,3072]{1,0:T(2,128)(2,1)} %b_down.3) | copy-start | bytes 36868
  0.7 13.7 %copy-start.6 = (bf16[2,2560]{1,0:T(2,128)(2,1)S(1)}, bf16[2,2560]{1,0:T(2,128)(2,1)}, u32[]{:S(2)}) copy-start(bf16[2,2560]{1,0:T(2,128)(2,1)} %rest_0_.3) | copy-start | bytes 30724
  14.4 37.8 %copy-start.7 = (s32[64]{0:T(128)S(1)}, s32[64]{0:T(128)}, u32[]{:S(2)}) copy-start(s32[64]{0:T(128)} %pos.3) | copy-start | bytes 772
